TPU v7x, 16 devices: a whole 2x2x2 slice. The times are simulated.
16 devices in a mesh: fsdp: 16 (over z, y, x, core).
Axes of the slice: x: 2, y: 2, z: 2, core: 2. Of those that a mesh axis runs over, the one named last changes fastest.
Arguments:
- h_saved: bfloat16 [3, 32768, 896], P(None, 'fsdp')
- g_out: bfloat16 [32768, 896], P('fsdp')
- w_gate: bfloat16 [3, 896, 4864], P(None, 'fsdp')
- w_up: bfloat16 [3, 896, 4864], P(None, 'fsdp')
- w_down: bfloat16 [3, 4864, 896], P(None, 'fsdp')
Outputs:
- output 1: float32 [3, 896, 4864], P(None, 'fsdp')
- output 2: float32 [3, 896, 4864], P(None, 'fsdp')
- output 3: float32 [3, 4864, 896], P(None, 'fsdp')
- output 4: bfloat16 [32768, 896], P('fsdp')
All inputs are finite; a program needn't handle non-finite values.
Results may differ from a plain program's by a relative error of at most 0.00587019.
Values are sent between devices in bfloat16 or wider.
A program may use at most 1 GiB of HBM per device.

v0:
```python
import jax
import jax.numpy as jnp
from jax import lax
from jax.sharding import PartitionSpec as P

EPS = 1e-6


def contract(lhs, rhs, lhs_dim, rhs_dim):
    return lax.dot_general(lhs, rhs, (((lhs_dim,), (rhs_dim,)), ((), ())), preferred_element_type=jnp.float32)


def block_backward(h_rows, g_rows, w_gate, w_up, w_down):
    hid_f32 = h_rows.astype(jnp.float32)
    inv_rms = lax.rsqrt(jnp.mean(hid_f32 * hid_f32, axis=-1, keepdims=True) + EPS)
    norm_f32 = hid_f32 * inv_rms
    normed = norm_f32.astype(jnp.bfloat16)
    gate_pre = contract(normed, w_gate, 1, 0)
    up_pre = contract(normed, w_up, 1, 0)
    gate_sig = jax.nn.sigmoid(gate_pre)
    gate_act = gate_pre * gate_sig
    hidden = (gate_act * up_pre).astype(jnp.bfloat16)
    d_hidden = contract(g_rows, w_down, 1, 1)
    grad_down = contract(hidden, g_rows, 0, 0)
    d_gate = (d_hidden * up_pre * gate_sig * (1.0 + gate_pre * (1.0 - gate_sig))).astype(jnp.bfloat16)
    d_up = (d_hidden * gate_act).astype(jnp.bfloat16)
    grad_gate = contract(normed, d_gate, 0, 0)
    grad_up = contract(normed, d_up, 0, 0)
    d_normed = contract(d_gate, w_gate, 1, 1) + contract(d_up, w_up, 1, 1)
    d_resid = inv_rms * (d_normed - norm_f32 * jnp.mean(d_normed * norm_f32, axis=-1, keepdims=True))
    g_next = (g_rows.astype(jnp.float32) + d_resid).astype(jnp.bfloat16)
    return g_next, grad_gate, grad_up, grad_down


def solution(mesh):
    weight_spec = P(None, 'fsdp', None)
    act_spec = P(None, 'fsdp', None)
    row_spec = P('fsdp', None)

    def local_backward(h_saved, g_out, w_gate, w_up, w_down):
        g_rows = g_out
        gate_list = []
        up_list = []
        down_list = []
        for layer_idx in reversed(range(h_saved.shape[0])):
            gate_full = lax.all_gather(w_gate[layer_idx], 'fsdp', axis=0, tiled=True)
            up_full = lax.all_gather(w_up[layer_idx], 'fsdp', axis=0, tiled=True)
            down_full = lax.all_gather(w_down[layer_idx], 'fsdp', axis=0, tiled=True)
            g_rows, grad_gate, grad_up, grad_down = block_backward(h_saved[layer_idx], g_rows, gate_full, up_full, down_full)
            gate_list.append(lax.psum_scatter(grad_gate, 'fsdp', scatter_dimension=0, tiled=True))
            up_list.append(lax.psum_scatter(grad_up, 'fsdp', scatter_dimension=0, tiled=True))
            down_list.append(lax.psum_scatter(grad_down, 'fsdp', scatter_dimension=0, tiled=True))
        return (jnp.stack(gate_list[::-1]), jnp.stack(up_list[::-1]), jnp.stack(down_list[::-1]), g_rows)

    return jax.shard_map(local_backward, mesh=mesh, in_specs=(act_spec, row_spec, weight_spec, weight_spec, weight_spec), out_specs=(weight_spec, weight_spec, weight_spec, row_spec), check_vma=False)
```

profile of v0, /device:TPU:0, one launch (start us, length us, event | category | flops | bytes accessed | tf_op | source)
XLA Modules:
  0.0 2152.0 jit_solution(4001236371091627677)
XLA Ops:
  18.1 7.9 fusion.96
  26.0 6.1 copy.15
  34.9 28.5 %all-gather.23.cloned.1.call-done = bf16[1,896,4864]{2,1,0:T(8,128)(2,1)} async-done(((bf16[1,56,4864]{2,1,0:T(8,128)(2,1)}), bf16[1,896,4864]{2,1,0:T(8,128)(2,1)}) %all-gather.23.cloned.1.call-update) | async-done | bytes 8716304 | tf_op jit(solution)/shard_map/all_gather | solution.py:46
  63.4 29.1 %fusion.37 = f32[2048,4864]{1,0:T(8,128)} fusion(bf16[1,896,4864]{2,1,0:T(8,128)(2,1)} %all-gather.23.cloned.1.call-done, bf16[1,2048,896]{1,2,0:T(8,128)(2,1)} %copy.15, f32[2048]{0:T(1024)S(1)} %add_rsqrt_fusion.1), kind=kOutput, calls=%fused_computation.55 | convolution fusion | flops 17856462848 | bytes 52240384 | tf_op jit(solution)/shard_map/dot_general | solution.py:10
  92.5 22.9 %all-gather.21.cloned.1.call-done = bf16[1,896,4864]{2,1,0:T(8,128)(2,1)} async-done(((bf16[1,56,4864]{2,1,0:T(8,128)(2,1)}), bf16[1,896,4864]{2,1,0:T(8,128)(2,1)}) %all-gather.21.cloned.1.call-update) | async-done | bytes 8716304 | tf_op jit(solution)/shard_map/all_gather | solution.py:47
  115.4 29.2 %fusion.41 = f32[2048,4864]{1,0:T(8,128)} fusion(bf16[1,896,4864]{2,1,0:T(8,128)(2,1)} %all-gather.21.cloned.1.call-done, bf16[1,2048,896]{1,2,0:T(8,128)(2,1)} %copy.15, f32[2048]{0:T(1024)S(1)} %add_rsqrt_fusion.1), kind=kOutput, calls=%fused_computation.59 | convolution fusion | flops 17856462848 | bytes 52240384 | tf_op jit(solution)/shard_map/dot_general | solution.py:10
  144.7 22.8 %all-gather.19.cloned.1.call-done = bf16[1,4864,896]{2,1,0:T(8,128)(2,1)} async-done(((bf16[1,304,896]{2,1,0:T(8,128)(2,1)}), bf16[1,4864,896]{2,1,0:T(8,128)(2,1)}) %all-gather.19.cloned.1.call-update) | async-done | bytes 8716304 | tf_op jit(solution)/shard_map/all_gather | solution.py:48
  167.5 51.4 %multiply_convert_fusion.7 = (bf16[2048,4864]{1,0:T(8,128)(2,1)}, bf16[2048,4864]{1,0:T(8,128)(2,1)}) fusion(f32[2048,4864]{1,0:T(8,128)} %fusion.37, f32[2048,4864]{1,0:T(8,128)} %fusion.41, bf16[2048,896]{1,0:T(8,128)(2,1)} %param.6, bf16[1,4864,896]{2,1,0:T(8,128)(2,1)} %all-gather.19.cloned.1.call-done), kind=kOutput, calls=%fused_computation.11 | convolution fusion | flops 17980456960 | bytes 131923968 | tf_op jit(solution)/shard_map/dot_general | solution.py:10
  218.9 25.1 %fusion.81 = f32[896,4864]{1,0:T(8,128)} fusion(bf16[2048,4864]{1,0:T(8,128)(2,1)} %get-tuple-element.12, bf16[1,2048,896]{1,2,0:T(8,128)(2,1)} %copy.15, f32[2048]{0:T(1024)S(1)} %add_rsqrt_fusion.1), kind=kOutput, calls=%fused_computation.89 | convolution fusion | flops 17856462848 | bytes 41033728 | tf_op jit(solution)/shard_map/dot_general | solution.py:10
  244.1 6.4 copy.10
  250.5 6.2 copy.16
  256.7 3.0 fusion.62
  259.7 25.2 %fusion.35 = f32[2048,896]{0,1:T(8,128)} fusion(bf16[2048,4864]{1,0:T(8,128)(2,1)} %get-tuple-element.13, bf16[1,896,4864]{2,1,0:T(8,128)(2,1)} %all-gather.23.cloned.1.call-done), kind=kOutput, calls=%fused_computation.53 | convolution fusion | flops 17850957824 | bytes 35979264 | tf_op jit(solution)/shard_map/dot_general | solution.py:10
  285.0 23.5 %fusion.51 = (f32[2048]{0:T(1024)S(1)}, f32[2048,896]{0,1:T(8,128)}) fusion(bf16[1,2048,896]{1,2,0:T(8,128)(2,1)S(1)} %copy-done.1, f32[2048]{0:T(1024)S(1)} %add_rsqrt_fusion.1, f32[2048,896]{0,1:T(8,128)} %fusion.35, bf16[2048,4864]{1,0:T(8,128)(2,1)} %get-tuple-element.12, bf16[1,896,4864]{2,1,0:T(8,128)(2,1)S(1)} %bitcast.126), kind=kOutput, calls=%fused_computation.69 | convolution fusion | flops 17860130816 | bytes 47005696 | tf_op jit(solution)/shard_map/dot_general | solution.py:10
  308.5 7.3 fusion.55
  315.8 29.4 %fusion.27 = f32[2048,4864]{1,0:T(8,128)} fusion(bf16[1,896,4864]{2,1,0:T(8,128)(2,1)} %all-gather.29.cloned.1.call-done, bf16[1,2048,896]{1,2,0:T(8,128)(2,1)} %copy.16, f32[2048]{0:T(1024)S(1)} %add_rsqrt_fusion), kind=kOutput, calls=%fused_computation.45 | convolution fusion | flops 17856462848 | bytes 52240384 | tf_op jit(solution)/shard_map/dot_general | solution.py:10
  345.2 29.2 %fusion.31 = f32[2048,4864]{1,0:T(8,128)} fusion(bf16[1,896,4864]{2,1,0:T(8,128)(2,1)} %all-gather.27.cloned.1.call-done, bf16[1,2048,896]{1,2,0:T(8,128)(2,1)} %copy.16, f32[2048]{0:T(1024)S(1)} %add_rsqrt_fusion), kind=kOutput, calls=%fused_computation.49 | convolution fusion | flops 17856462848 | bytes 52240384 | tf_op jit(solution)/shard_map/dot_general | solution.py:10
  374.4 51.8 %multiply_convert_fusion.5 = (bf16[2048,4864]{1,0:T(8,128)(2,1)}, bf16[2048,4864]{1,0:T(8,128)(2,1)}) fusion(f32[2048,4864]{1,0:T(8,128)} %fusion.27, f32[2048,4864]{1,0:T(8,128)} %fusion.31, bf16[2048,896]{0,1:T(8,128)(2,1)} %fusion.55, bf16[1,4864,896]{2,1,0:T(8,128)(2,1)} %all-gather.25.cloned.1.call-done), kind=kOutput, calls=%fused_computation.7 | convolution fusion | flops 17980456960 | bytes 131923968 | tf_op jit(solution)/shard_map/dot_general | solution.py:10
  426.2 25.1 %fusion.87 = f32[896,4864]{1,0:T(8,128)} fusion(bf16[2048,4864]{1,0:T(8,128)(2,1)} %get-tuple-element.10, bf16[1,2048,896]{1,2,0:T(8,128)(2,1)} %copy.16, f32[2048]{0:T(1024)S(1)} %add_rsqrt_fusion), kind=kOutput, calls=%fused_computation.91 | convolution fusion | flops 17856462848 | bytes 41033728 | tf_op jit(solution)/shard_map/dot_general | solution.py:10
  451.4 6.6 copy.14
  458.0 3.0 fusion.50
  461.0 25.2 %fusion.25 = f32[2048,896]{0,1:T(8,128)} fusion(bf16[2048,4864]{1,0:T(8,128)(2,1)} %get-tuple-element.11, bf16[1,896,4864]{2,1,0:T(8,128)(2,1)} %all-gather.29.cloned.1.call-done), kind=kOutput, calls=%fused_computation.43 | convolution fusion | flops 17850957824 | bytes 35979264 | tf_op jit(solution)/shard_map/dot_general | solution.py:10
  486.3 23.5 %fusion.57 = (f32[2048]{0:T(1024)S(1)}, f32[2048,896]{0,1:T(8,128)}) fusion(bf16[1,2048,896]{1,2,0:T(8,128)(2,1)S(1)} %copy-done.2, f32[2048]{0:T(1024)S(1)} %add_rsqrt_fusion, f32[2048,896]{0,1:T(8,128)} %fusion.25, bf16[2048,4864]{1,0:T(8,128)(2,1)} %get-tuple-element.10, bf16[1,896,4864]{2,1,0:T(8,128)(2,1)S(1)} %bitcast.124), kind=kOutput, calls=%fused_computation.75 | convolution fusion | flops 17860130816 | bytes 47005696 | tf_op jit(solution)/shard_map/dot_general | solution.py:10
  509.8 7.3 fusion.61
  517.1 29.4 %fusion.17 = f32[2048,4864]{1,0:T(8,128)} fusion(bf16[1,896,4864]{2,1,0:T(8,128)(2,1)} %all-gather.35.cloned.1.call-done, bf16[1,2048,896]{1,2,0:T(8,128)(2,1)} %copy.14, f32[2048]{0:T(1024)S(1)} %add_rsqrt_fusion.2), kind=kOutput, calls=%fused_computation.35 | convolution fusion | flops 17856462848 | bytes 52240384 | tf_op jit(solution)/shard_map/dot_general | solution.py:10
  546.5 29.1 %fusion.21 = f32[2048,4864]{1,0:T(8,128)} fusion(bf16[1,896,4864]{2,1,0:T(8,128)(2,1)} %all-gather.33.cloned.1.call-done, bf16[1,2048,896]{1,2,0:T(8,128)(2,1)} %copy.14, f32[2048]{0:T(1024)S(1)} %add_rsqrt_fusion.2), kind=kOutput, calls=%fused_computation.39 | convolution fusion | flops 17856462848 | bytes 52240384 | tf_op jit(solution)/shard_map/dot_general | solution.py:10
  575.7 51.9 %multiply_convert_fusion.3 = (bf16[2048,4864]{1,0:T(8,128)(2,1)}, bf16[2048,4864]{1,0:T(8,128)(2,1)}) fusion(f32[2048,4864]{1,0:T(8,128)} %fusion.17, f32[2048,4864]{1,0:T(8,128)} %fusion.21, bf16[2048,896]{0,1:T(8,128)(2,1)} %fusion.61, bf16[1,4864,896]{2,1,0:T(8,128)(2,1)} %all-gather.31.cloned.1.call-done), kind=kOutput, calls=%fused_computation.3 | convolution fusion | flops 17980456960 | bytes 131923968 | tf_op jit(solution)/shard_map/dot_general | solution.py:10
  627.5 25.2 %fusion.75 = f32[896,4864]{1,0:T(8,128)} fusion(bf16[2048,4864]{1,0:T(8,128)(2,1)} %get-tuple-element.8, bf16[1,2048,896]{1,2,0:T(8,128)(2,1)} %copy.14, f32[2048]{0:T(1024)S(1)} %add_rsqrt_fusion.2), kind=kOutput, calls=%fused_computation.87 | convolution fusion | flops 17856462848 | bytes 41033728 | tf_op jit(solution)/shard_map/dot_general | solution.py:10
  653.4 25.2 %fusion.83 = f32[896,4864]{1,0:T(8,128)} fusion(bf16[2048,4864]{1,0:T(8,128)(2,1)} %get-tuple-element.13, bf16[1,2048,896]{1,2,0:T(8,128)(2,1)} %copy.15, f32[2048]{0:T(1024)S(1)} %copy-done.10), kind=kOutput, calls=%fused_computation.90 | convolution fusion | flops 17856462848 | bytes 41033728 | tf_op jit(solution)/shard_map/dot_general | solution.py:10
  679.3 25.6 %fusion.89 = f32[896,4864]{1,0:T(8,128)} fusion(bf16[2048,4864]{1,0:T(8,128)(2,1)} %get-tuple-element.11, bf16[1,2048,896]{1,2,0:T(8,128)(2,1)} %copy.16, f32[2048]{0:T(1024)S(1)} %copy-done.12), kind=kOutput, calls=%fused_computation.92 | convolution fusion | flops 17856462848 | bytes 41033728 | tf_op jit(solution)/shard_map/dot_general | solution.py:10
  705.0 25.1 %fusion.77 = f32[896,4864]{1,0:T(8,128)} fusion(bf16[2048,4864]{1,0:T(8,128)(2,1)} %get-tuple-element.9, bf16[1,2048,896]{1,2,0:T(8,128)(2,1)} %copy.14, f32[2048]{0:T(1024)S(1)} %add_rsqrt_fusion.2), kind=kOutput, calls=%fused_computation.88 | convolution fusion | flops 17856462848 | bytes 41033728 | tf_op jit(solution)/shard_map/dot_general | solution.py:10
  730.2 38.1 %fusion.5 = f32[4864,896]{1,0:T(8,128)} fusion(bf16[2048,896]{1,0:T(8,128)(2,1)} %param.6, f32[2048,4864]{1,0:T(8,128)} %fusion.41, f32[2048,4864]{1,0:T(8,128)} %fusion.37), kind=kOutput, calls=%fused_computation.17 | convolution fusion | flops 17910726656 | bytes 100794368 | tf_op jit(solution)/shard_map/dot_general | solution.py:10
  768.4 37.2 %fusion.4 = f32[4864,896]{1,0:T(8,128)} fusion(bf16[2048,896]{0,1:T(8,128)(2,1)} %fusion.55, f32[2048,4864]{1,0:T(8,128)} %fusion.31, f32[2048,4864]{1,0:T(8,128)} %fusion.27), kind=kOutput, calls=%fused_computation.16 | convolution fusion | flops 17910726656 | bytes 100794368 | tf_op jit(solution)/shard_map/dot_general | solution.py:10
  805.6 37.4 %fusion.3 = f32[4864,896]{1,0:T(8,128)} fusion(bf16[2048,896]{0,1:T(8,128)(2,1)} %fusion.61, f32[2048,4864]{1,0:T(8,128)} %fusion.21, f32[2048,4864]{1,0:T(8,128)} %fusion.17), kind=kOutput, calls=%fused_computation.15 | convolution fusion | flops 17910726656 | bytes 100794368 | tf_op jit(solution)/shard_map/dot_general | solution.py:10
  843.1 23.9 %fusion.15 = f32[2048,896]{0,1:T(8,128)S(1)} fusion(bf16[2048,4864]{1,0:T(8,128)(2,1)} %get-tuple-element.9, bf16[1,896,4864]{2,1,0:T(8,128)(2,1)} %all-gather.35.cloned.1.call-done), kind=kOutput, calls=%fused_computation.33 | convolution fusion | flops 17850957824 | bytes 35979264 | tf_op jit(solution)/shard_map/dot_general | solution.py:10
  867.0 25.5 %fusion.45 = (f32[2048]{0:T(1024)S(1)}, f32[2048,896]{0,1:T(8,128)}) fusion(bf16[1,2048,896]{1,2,0:T(8,128)(2,1)S(1)} %copy-done, f32[2048]{0:T(1024)S(1)} %copy-done.8, f32[2048,896]{0,1:T(8,128)S(1)} %fusion.15, bf16[2048,4864]{1,0:T(8,128)(2,1)} %get-tuple-element.8, bf16[1,896,4864]{2,1,0:T(8,128)(2,1)} %all-gather.33.cloned.1.call-done), kind=kOutput, calls=%fused_computation.63 | convolution fusion | flops 17860130816 | bytes 47005696 | tf_op jit(solution)/shard_map/dot_general | solution.py:10
  892.6 7.3 fusion.49
  899.9 6.0 copy.13
  905.9 129.2 %reduce-scatter.16.cloned.1.call-done = f32[56,4864]{1,0:T(8,128)} async-done(((f32[896,4864]{1,0:T(8,128)}), f32[56,4864]{1,0:T(8,128)}) %reduce-scatter.16.cloned.1.call-update) | async-done | bytes 1089552 | tf_op jit(solution)/shard_map/reduce_scatter | solution.py:51
  1035.1 3.8 pad_maximum_fusion.1
  1038.9 180.6 %reduce-scatter.14.cloned.1.call-done = f32[56,4864]{1,0:T(8,128)} async-done(((f32[896,4864]{1,0:T(8,128)}), f32[56,4864]{1,0:T(8,128)}) %reduce-scatter.14.cloned.1.call-update) | async-done | bytes 1089552 | tf_op jit(solution)/shard_map/reduce_scatter | solution.py:50
  1219.6 184.3 %reduce-scatter.12.cloned.1.call-done = f32[56,4864]{1,0:T(8,128)} async-done(((f32[896,4864]{1,0:T(8,128)}), f32[56,4864]{1,0:T(8,128)}) %reduce-scatter.12.cloned.1.call-update) | async-done | bytes 1089552 | tf_op jit(solution)/shard_map/reduce_scatter | solution.py:50
  1403.9 184.3 %reduce-scatter.10.cloned.1.call-done = f32[56,4864]{1,0:T(8,128)} async-done(((f32[896,4864]{1,0:T(8,128)}), f32[56,4864]{1,0:T(8,128)}) %reduce-scatter.10.cloned.1.call-update) | async-done | bytes 1089552 | tf_op jit(solution)/shard_map/reduce_scatter | solution.py:50
  1588.2 3.8 pad_maximum_fusion
  1592.0 180.5 %reduce-scatter.26.cloned.1.call-done = f32[304,896]{1,0:T(8,128)} async-done(((f32[4864,896]{1,0:T(8,128)}), f32[304,896]{1,0:T(8,128)}) %reduce-scatter.26.cloned.1.call-update) | async-done | bytes 1089552 | tf_op jit(solution)/shard_map/reduce_scatter | solution.py:52
  1772.4 184.3 %reduce-scatter.24.cloned.1.call-done = f32[304,896]{1,0:T(8,128)} async-done(((f32[4864,896]{1,0:T(8,128)}), f32[304,896]{1,0:T(8,128)}) %reduce-scatter.24.cloned.1.call-update) | async-done | bytes 1089552 | tf_op jit(solution)/shard_map/reduce_scatter | solution.py:52
  1956.7 184.3 %reduce-scatter.22.cloned.1.call-done = f32[304,896]{1,0:T(8,128)} async-done(((f32[4864,896]{1,0:T(8,128)}), f32[304,896]{1,0:T(8,128)}) %reduce-scatter.22.cloned.1.call-update) | async-done | bytes 1089552 | tf_op jit(solution)/shard_map/reduce_scatter | solution.py:52
  2141.0 3.8 pad_maximum_fusion.2
  (94 shorter events, 15.4 us)
Async XLA Ops:
  7.2 5.6 copy-start.6
  7.2 56.2 %all-gather.23.cloned.1.call-start = ((), (), s32[]{:S(2)}) async-start(), calls=%async_computation.20 | async-start | bytes 9261056 | tf_op jit(solution)/shard_map/all_gather | solution.py:46
  9.9 105.5 %all-gather.21.cloned.1.call-start = ((), (), s32[]{:S(2)}) async-start(), calls=%async_computation.19 | async-start | bytes 9261056 | tf_op jit(solution)/shard_map/all_gather | solution.py:47
  12.7 154.8 %all-gather.19.cloned.1.call-start = ((), (), s32[]{:S(2)}) async-start(), calls=%async_computation.18 | async-start | bytes 9261056 | tf_op jit(solution)/shard_map/all_gather | solution.py:48
  14.0 301.7 %all-gather.29.cloned.1.call-start = ((), (), s32[]{:S(2)}) async-start(), calls=%async_computation.23 | async-start | bytes 9261056 | tf_op jit(solution)/shard_map/all_gather | solution.py:46
  14.6 330.6 %all-gather.27.cloned.1.call-start = ((), (), s32[]{:S(2)}) async-start(), calls=%async_computation.22 | async-start | bytes 9261056 | tf_op jit(solution)/shard_map/all_gather | solution.py:47
  15.2 359.2 %all-gather.25.cloned.1.call-start = ((), (), s32[]{:S(2)}) async-start(), calls=%async_computation.21 | async-start | bytes 9261056 | tf_op jit(solution)/shard_map/all_gather | solution.py:48
  15.8 501.3 %all-gather.35.cloned.1.call-start = ((), (), s32[]{:S(2)}) async-start(), calls=%async_computation.26 | async-start | bytes 9261056 | tf_op jit(solution)/shard_map/all_gather | solution.py:46
  16.5 530.0 %all-gather.33.cloned.1.call-start = ((), (), s32[]{:S(2)}) async-start(), calls=%async_computation.25 | async-start | bytes 9261056 | tf_op jit(solution)/shard_map/all_gather | solution.py:47
  17.3 558.4 %all-gather.31.cloned.1.call-start = ((), (), s32[]{:S(2)}) async-start(), calls=%async_computation.24 | async-start | bytes 9261056 | tf_op jit(solution)/shard_map/all_gather | solution.py:48
  18.0 887.9 %reduce-scatter.20.cloned.1.call-start = ((), (), s32[]{:S(2)}) async-start(), calls=%async_computation.14 | async-start | bytes 18522112 | tf_op jit(solution)/shard_map/reduce_scatter | solution.py:51
  34.9 273.6 %copy-start.9 = (f32[2048]{0:T(1024)}, f32[2048]{0:T(1024)S(1)}, u32[]{:S(2)}) copy-start(f32[2048]{0:T(1024)S(1)} %add_rsqrt_fusion.1) | copy-start | bytes 24580
  244.1 661.9 %reduce-scatter.18.cloned.1.call-start = ((), (), s32[]{:S(2)}) async-start(), calls=%async_computation.13 | async-start | bytes 18522112 | tf_op jit(solution)/shard_map/reduce_scatter | solution.py:51
  256.7 28.2 %slice-start.3 = ((s8[8716288]{0:T(1024)(128)(4,1)}), s8[4194304]{0:T(1024)(128)(4,1)S(1)}, s32[]{:S(2)}) async-start(s8[8716288]{0:T(1024)(128)(4,1)} %bitcast.125), calls=%async_computation.30 | async-start | bytes 8388608
  259.7 250.1 %copy-start.11 = (f32[2048]{0:T(1024)}, f32[2048]{0:T(1024)S(1)}, u32[]{:S(2)}) copy-start(f32[2048]{0:T(1024)S(1)} %add_rsqrt_fusion) | copy-start | bytes 24580
  259.7 25.2 %copy-start.1 = (bf16[1,2048,896]{1,2,0:T(8,128)(2,1)S(1)}, bf16[1,2048,896]{1,2,0:T(8,128)(2,1)}, u32[]{:S(2)}) copy-start(bf16[1,2048,896]{1,2,0:T(8,128)(2,1)} %copy.15) | copy-start | bytes 11010052
  259.7 25.2 %slice-start.4 = ((s8[8716288]{0:T(1024)(128)(4,1)}), s8[4194304]{0:T(1024)(128)(4,1)S(1)}, s32[]{:S(2)}) async-start(s8[8716288]{0:T(1024)(128)(4,1)} %bitcast.125), calls=%async_computation.31 | async-start | bytes 8388608
  259.7 25.2 %slice-start.5 = ((s8[8716288]{0:T(1024)(128)(4,1)}), s8[327680]{0:T(1024)(128)(4,1)S(1)}, s32[]{:S(2)}) async-start(s8[8716288]{0:T(1024)(128)(4,1)} %bitcast.125), calls=%async_computation.32 | async-start | bytes 655360
  285.0 23.5 %copy-start.3 = (bf16[2048,896]{0,1:T(8,128)(2,1)S(1)}, bf16[2048,896]{0,1:T(8,128)(2,1)}, u32[]{:S(2)}) copy-start(bf16[2048,896]{0,1:T(8,128)(2,1)} %copy.10) | copy-start | bytes 11010052
  451.3 583.8 %reduce-scatter.16.cloned.1.call-start = ((), (), s32[]{:S(2)}) async-start(), calls=%async_computation.12 | async-start | bytes 18522112 | tf_op jit(solution)/shard_map/reduce_scatter | solution.py:51
  458.0 28.2 %slice-start = ((s8[8716288]{0:T(1024)(128)(4,1)}), s8[4194304]{0:T(1024)(128)(4,1)S(1)}, s32[]{:S(2)}) async-start(s8[8716288]{0:T(1024)(128)(4,1)} %bitcast.123), calls=%async_computation.27 | async-start | bytes 8388608
  461.0 244.0 %copy-start.7 = (f32[2048]{0:T(1024)}, f32[2048]{0:T(1024)S(1)}, u32[]{:S(2)}) copy-start(f32[2048]{0:T(1024)S(1)} %add_rsqrt_fusion.2) | copy-start | bytes 24580
  461.0 25.2 %copy-start.2 = (bf16[1,2048,896]{1,2,0:T(8,128)(2,1)S(1)}, bf16[1,2048,896]{1,2,0:T(8,128)(2,1)}, u32[]{:S(2)}) copy-start(bf16[1,2048,896]{1,2,0:T(8,128)(2,1)} %copy.16) | copy-start | bytes 11010052
  461.0 25.2 %slice-start.1 = ((s8[8716288]{0:T(1024)(128)(4,1)}), s8[4194304]{0:T(1024)(128)(4,1)S(1)}, s32[]{:S(2)}) async-start(s8[8716288]{0:T(1024)(128)(4,1)} %bitcast.123), calls=%async_computation.28 | async-start | bytes 8388608
  461.0 25.2 %slice-start.2 = ((s8[8716288]{0:T(1024)(128)(4,1)}), s8[327680]{0:T(1024)(128)(4,1)S(1)}, s32[]{:S(2)}) async-start(s8[8716288]{0:T(1024)(128)(4,1)} %bitcast.123), calls=%async_computation.29 | async-start | bytes 655360
  486.3 23.5 %copy-start.4 = (bf16[2048,896]{0,1:T(8,128)(2,1)S(1)}, bf16[2048,896]{0,1:T(8,128)(2,1)}, u32[]{:S(2)}) copy-start(bf16[2048,896]{0,1:T(8,128)(2,1)} %fusion.55) | copy-start | bytes 11010052
  652.7 0.7 copy-start.10
  652.7 566.9 %reduce-scatter.14.cloned.1.call-start = ((), (), s32[]{:S(2)}) async-start(), calls=%async_computation.11 | async-start | bytes 18522112 | tf_op jit(solution)/shard_map/reduce_scatter | solution.py:50
  678.6 0.7 copy-start.12
  678.6 725.2 %reduce-scatter.12.cloned.1.call-start = ((), (), s32[]{:S(2)}) async-start(), calls=%async_computation.10 | async-start | bytes 18522112 | tf_op jit(solution)/shard_map/reduce_scatter | solution.py:50
  704.9 883.2 %reduce-scatter.10.cloned.1.call-start = ((), (), s32[]{:S(2)}) async-start(), calls=%async_computation.9 | async-start | bytes 18522112 | tf_op jit(solution)/shard_map/reduce_scatter | solution.py:50
  730.1 1042.3 %reduce-scatter.26.cloned.1.call-start = ((), (), s32[]{:S(2)}) async-start(), calls=%async_computation.17 | async-start | bytes 18522112 | tf_op jit(solution)/shard_map/reduce_scatter | solution.py:52
  768.3 1188.4 %reduce-scatter.24.cloned.1.call-start = ((), (), s32[]{:S(2)}) async-start(), calls=%async_computation.16 | async-start | bytes 18522112 | tf_op jit(solution)/shard_map/reduce_scatter | solution.py:52
  805.6 1335.4 %reduce-scatter.22.cloned.1.call-start = ((), (), s32[]{:S(2)}) async-start(), calls=%async_computation.15 | async-start | bytes 18522112 | tf_op jit(solution)/shard_map/reduce_scatter | solution.py:52
  843.1 23.9 %copy-start = (bf16[1,2048,896]{1,2,0:T(8,128)(2,1)S(1)}, bf16[1,2048,896]{1,2,0:T(8,128)(2,1)}, u32[]{:S(2)}) copy-start(bf16[1,2048,896]{1,2,0:T(8,128)(2,1)} %copy.14) | copy-start | bytes 11010052
  843.1 23.9 %copy-start.8 = (f32[2048]{0:T(1024)S(1)}, f32[2048]{0:T(1024)}, u32[]{:S(2)}) copy-start(f32[2048]{0:T(1024)} %copy-done.7) | copy-start | bytes 24580
  867.0 25.6 %copy-start.5 = (bf16[2048,896]{0,1:T(8,128)(2,1)S(1)}, bf16[2048,896]{0,1:T(8,128)(2,1)}, u32[]{:S(2)}) copy-start(bf16[2048,896]{0,1:T(8,128)(2,1)} %fusion.61) | copy-start | bytes 11010052
Sparse Core Ops, SparseCore 0:
  10.8 52.5 all-gather.22
  65.6 49.7 all-gather.20
  117.7 49.7 all-gather.18
  170.1 49.7 all-gather.28
  222.0 49.7 all-gather.26
  273.9 49.7 all-gather.24
  326.5 49.7 all-gather.34
  378.5 49.7 all-gather.32
  430.5 49.7 all-gather.30
  482.5 183.8 reduce-scatter.19
  668.7 182.1 reduce-scatter.17
  853.0 182.0 reduce-scatter.15
  1037.4 182.1 reduce-scatter.13
  1221.7 182.0 reduce-scatter.11
  1406.0 182.1 reduce-scatter.9
  1590.3 182.0 reduce-scatter.25
  1774.6 182.1 reduce-scatter.23
  1958.9 182.0 reduce-scatter.21
where the time goes:
time: 2160 us; the launch traced here: 2150 us
  waiting for transfers between devices  1310 us (61%)
  matrix products  742 us (34%)
  local copies, waits for them, and re-layouts  47.3 us (2%)
  other arithmetic  42.1 us (2%)
    dot_general x24, matrix products, contract(): lax.dot_general(lhs, rhs, (((lhs_dim,), (rhs_dim,)), ((), ())), preferred...  742 us
    reduce_scatter x3, waiting for transfers between devices, local_backward(): lax.psum_scatter(grad_gate, 'fsdp', scatter_dimension=0, tiled=True)  549 us
    reduce_scatter x3, waiting for transfers between devices, local_backward(): lax.psum_scatter(grad_down, 'fsdp', scatter_dimension=0, tiled=True)  549 us
    reduce_scatter x3, waiting for transfers between devices, local_backward(): lax.psum_scatter(grad_up, 'fsdp', scatter_dimension=0, tiled=True)  129 us
  transfers between devices with their start and end apart: 18, of which 10 were waited for; matrix products, arithmetic and copies ran while one was open for 38% of the time, Pallas kernels for 0%

commit v1 on v0

v1 whole, which is shorter than its diff:
```python
import jax
import jax.numpy as jnp
from jax import lax
from jax.experimental import pallas as pl
from jax.experimental.pallas import tpu as pltpu
from jax.sharding import PartitionSpec as P

EPS = 1e-6
LAYERS = 3
D = 896
FF = 4864
ROWS = 2048
DEV = 16
DS = D // DEV
FS = FF // DEV
CPD = 16
CH = CPD * DEV
NC = FF // CH
NK = NC * LAYERS
LEAD = 4
TAIL = 5
WS = 6
RB = 1024
BB = 256
HALF = CH // 2
MESH = pl.DeviceIdType.MESH
BF = jnp.bfloat16
F32 = jnp.float32


def dot(a, b, ca, cb):
    return lax.dot_general(a, b, (((ca,), (cb,)), ((), ())), preferred_element_type=F32)


def kernel(h_hbm, g_hbm, w1_hbm, w3_hbm, w2_hbm,
           o1_hbm, o3_hbm, o2_hbm, og_hbm,
           n_v, nt_v, g_v, gt_v, dn_v, h_v, a_v, d_v,
           w1_v, w3_v, w2_v,
           g1_v, g3_v, g2_v,
           rd1, rd3, rd2, ra1, ra3, ra2, rb1, rb3, rb2, rc1, rc3, rc2,
           pa1, pa3, pa2, pb1, pb3, pb2, s1, s3, s2,
           ag_send, ag_recv, rs_send, rs_recv, own_sem, out_sem, h_sem, g_sem):
    me = lax.axis_index('fsdp')
    c = me % 2
    x = (me // 2) % 2
    y = (me // 4) % 2
    z = (me // 8) % 2
    core = me + 1 - 2 * c
    nx = me + 2 - 4 * x
    ny = me + 4 - 8 * y
    nz = me + 8 - 16 * z

    barrier = pltpu.get_barrier_semaphore()
    for peer in (core, nx, ny, nz):
        pl.semaphore_signal(barrier, inc=1, device_id=(peer,), device_id_type=MESH)
    pl.semaphore_wait(barrier, 4)

    weights = (w1_v, w3_v, w2_v)
    grads = (g1_v, g3_v, g2_v)
    rds, ras, rbs, rcs = (rd1, rd3, rd2), (ra1, ra3, ra2), (rb1, rb3, rb2), (rc1, rc3, rc2)
    pas, pbs, outs = (pa1, pa3, pa2), (pb1, pb3, pb2), (s1, s3, s2)
    order = ((nx, ny, nz), (ny, nz, nx), (nz, nx, ny))

    def gather_slice(m, stage, k):
        s = lax.rem(k, WS)
        w = weights[m]
        if m == 0:
            return (w.at[s, c, z, y, x], w.at[s, c, z, y], w.at[s, c, z], w.at[s, c])[stage]
        if m == 1:
            return (w.at[s, c, z, y, x], w.at[s, c, z, :, x], w.at[s, c, :, :, x], w.at[s, c])[stage]
        return (w.at[s, z, y, x, c], w.at[s, :, y, x, c], w.at[s, :, y, :, c], w.at[s, :, :, :, c])[stage]

    def own_block(m, k):
        layer = LAYERS - 1 - k // NC
        i = lax.rem(k, NC)
        if m == 2:
            return w2_hbm.at[layer, pl.ds(pl.multiple_of(i * CPD, CPD), CPD)]
        return (w1_hbm, w3_hbm)[m].at[layer, i]

    def gather_copy(m, stage, k):
        par = lax.rem(k, 2)
        dst = gather_slice(m, stage, k)
        src = own_block(m, k) if stage == 0 else dst
        peer = core if stage == 3 else order[m][stage]
        return pltpu.make_async_remote_copy(
            src_ref=src, dst_ref=dst, send_sem=ag_send.at[m, stage, par], recv_sem=ag_recv.at[m, stage, par],
            device_id=(peer,), device_id_type=MESH)

    def own_copy(m, k):
        return pltpu.make_async_copy(own_block(m, k), gather_slice(m, 0, k), own_sem.at[m])

    def reduce_copy(m, stage, k):
        par = lax.rem(k, 2)
        g, pa, pb = grads[m], pas[m], pbs[m]
        if stage == 0:
            src, dst, peer = g.at[par, :, :, :, 1 - c], rds[m].at[par], core
        elif stage == 1:
            src = (g.at[par, :, :, 1 - x, c], g.at[par, :, 1 - y, :, c], g.at[par, 1 - z, :, :, c])[m]
            dst, peer = ras[m].at[par], order[m][0]
        elif stage == 2:
            src = (pa.at[:, 1 - y], pa.at[1 - z], pa.at[:, 1 - x])[m]
            dst, peer = rbs[m].at[par], order[m][1]
        else:
            src = (pb.at[1 - z], pb.at[1 - x], pb.at[1 - y])[m]
            dst, peer = rcs[m].at[par], order[m][2]
        return pltpu.make_async_remote_copy(
            src_ref=src, dst_ref=dst, send_sem=rs_send.at[m, stage, par], recv_sem=rs_recv.at[m, stage, par],
            device_id=(peer,), device_id_type=MESH)

    def out_copy(m, k):
        layer = LAYERS - 1 - k // NC
        i = lax.rem(k, NC)
        if m == 2:
            dst = o2_hbm.at[layer, pl.ds(pl.multiple_of(i * CPD, CPD), CPD)]
        else:
            dst = (o1_hbm, o3_hbm)[m].at[layer, i]
        return pltpu.make_async_copy(outs[m], dst, out_sem.at[m])

    def h_copy(li):
        return pltpu.make_async_copy(h_hbm.at[LAYERS - 1 - li], h_v.at[lax.rem(li, 2)], h_sem.at[lax.rem(li, 2)])

    def g_copy():
        return pltpu.make_async_copy(g_hbm, g_v, g_sem)

    def finalize_rows(li, r0):
        rows = pl.ds(r0, BB)
        hf = h_v[lax.rem(li, 2), rows, :].astype(F32)
        r = lax.rsqrt(jnp.mean(hf * hf, axis=-1, keepdims=True) + EPS)
        m = hf * r
        dn = dn_v[rows, :]
        dr = r * (dn - m * jnp.mean(dn * m, axis=-1, keepdims=True))
        g_v[rows, :] = (g_v[rows, :].astype(F32) + dr).astype(BF)

    def prepare_rows(li, r0):
        rows = pl.ds(r0, BB)
        hf = h_v[lax.rem(li, 2), rows, :].astype(F32)
        r = lax.rsqrt(jnp.mean(hf * hf, axis=-1, keepdims=True) + EPS)
        nb = (hf * r).astype(BF)
        n_v[rows, :] = nb
        nt_v[:, rows] = nb.T
        gt_v[:, rows] = g_v[rows, :].T
        dn_v[rows, :] = jnp.zeros((BB, D), F32)

    def gather_step(k):
        @pl.when((k >= 0) & (k < NK))
        def _():
            for m in range(3):
                gather_copy(m, 3, k).wait()

        for lag, stage in ((1, 2), (2, 1), (3, 0)):
            @pl.when((k + lag >= 0) & (k + lag < NK))
            def _():
                for m in range(3):
                    gather_copy(m, stage, k + lag).wait()
                    if stage == 0:
                        own_copy(m, k + lag).wait()

        for lag, stage in ((1, 3), (2, 2), (3, 1), (4, 0)):
            @pl.when((k + lag >= 0) & (k + lag < NK))
            def _():
                for m in range(3):
                    gather_copy(m, stage, k + lag).start()
                    if stage == 0:
                        own_copy(m, k + lag).start()

        @pl.when((k >= 1) & (k <= NK))
        def _():
            for m in range(3):
                reduce_copy(m, 0, k - 1).start()

    def reduce_step(k):
        def live(lag):
            return (k - lag >= 0) & (k - lag < NK)

        @pl.when(live(4))
        def _():
            kf = k - 4
            par = lax.rem(kf, 2)

            @pl.when(kf >= 1)
            def _():
                for m in range(3):
                    out_copy(m, kf - 1).wait()
            for m in range(3):
                reduce_copy(m, 3, kf).wait()
                keep = (z, x, y)[m]
                outs[m][...] = rcs[m][par] + pbs[m][keep]
                out_copy(m, kf).start()

        @pl.when(live(3))
        def _():
            kf = k - 3
            par = lax.rem(kf, 2)
            for m in range(3):
                reduce_copy(m, 2, kf).wait()
                for a in range(2):
                    kept = (lambda: pa1[a, y], lambda: pa3[z, a], lambda: pa2[a, x])[m]()
                    pbs[m][a] = rbs[m][par, a] + kept

        @pl.when(live(2))
        def _():
            kf = k - 2
            par = lax.rem(kf, 2)
            for m in range(3):
                reduce_copy(m, 1, kf).wait()
                for a in range(2):
                    for b in range(2):
                        kept = (lambda: g1_v[par, a, b, x, c], lambda: g3_v[par, a, y, b, c], lambda: g2_v[par, z, a, b, c])[m]()
                        pas[m][a, b] = ras[m][par, a, b] + kept

        @pl.when(live(1))
        def _():
            kf = k - 1
            par = lax.rem(kf, 2)
            for m in range(3):
                reduce_copy(m, 0, kf).wait()
                for a in range(2):
                    for b in range(2):
                        for d in range(2):
                            grads[m][par, a, b, d, c] = grads[m][par, a, b, d, c] + rds[m][par, a, b, d]

        for lag, stage in ((3, 3), (2, 2), (1, 1)):
            @pl.when(live(lag))
            def _():
                for m in range(3):
                    reduce_copy(m, stage, k - lag).start()

    def row_phase(k):
        s = lax.rem(k, WS)

        def body(b, carry):
            rows = pl.ds(pl.multiple_of(b * RB, RB), RB)
            w1 = jnp.concatenate([w1_v[s, 0].reshape(D, HALF), w1_v[s, 1].reshape(D, HALF)], axis=1)
            w3 = jnp.concatenate([w3_v[s, 0].reshape(D, HALF), w3_v[s, 1].reshape(D, HALF)], axis=1)
            w2 = w2_v[s].reshape(CH, D)
            nb = n_v[rows, :]
            u = dot(nb, w1, 1, 0)
            v = dot(nb, w3, 1, 0)
            da = jnp.concatenate([dot(g_v[pl.ds(pl.multiple_of(b * RB + q * (RB // 2), RB // 2), RB // 2), :], w2, 1, 1) for q in range(2)], axis=0)
            sig = 1.0 / (1.0 + jnp.exp(-u))
            act = u * sig
            a_v[rows, :] = (act * v).astype(BF)
            du = (da * v * sig * (1.0 + u * (1.0 - sig))).astype(BF)
            dv = (da * act).astype(BF)
            d_v[rows, pl.ds(0, CH)] = du
            d_v[rows, pl.ds(CH, CH)] = dv
            for q in range(2):
                rq = slice(q * (RB // 2), (q + 1) * (RB // 2))
                rr = pl.ds(pl.multiple_of(b * RB + q * (RB // 2), RB // 2), RB // 2)
                dn_v[rr, :] += dot(du[rq], w1, 1, 1) + dot(dv[rq], w3, 1, 1)
            return carry

        lax.fori_loop(0, ROWS // RB, body, 0)

    def grad_phase(k):
        par = lax.rem(k, 2)
        nt = nt_v[...]
        g1_v[par] = dot(nt, d_v[:, pl.ds(0, CH)], 1, 0).reshape(2, 2, 2, 2, DS, CH)
        g3_v[par] = dot(nt, d_v[:, pl.ds(CH, CH)], 1, 0).reshape(2, 2, 2, 2, DS, CH)
        g2_v[par] = dot(gt_v[...], a_v[...], 1, 0).T.reshape(2, 2, 2, 2, CPD, D)

    h_copy(0).start()
    g_copy().start()
    h_copy(1).start()

    def step(t, carry):
        k = t - LEAD

        @pl.when(t == 0)
        def _():
            pass

        @pl.when((k == NC) | (k == 2 * NC) | (k == NK))
        def _():
            li = k // NC

            def rows(b, cc):
                finalize_rows(li - 1, pl.multiple_of(b * BB, BB))
                return cc
            lax.fori_loop(0, ROWS // BB, rows, 0)

            @pl.when(li < LAYERS)
            def _():
                h_copy(li).wait()

                def rows2(b, cc):
                    prepare_rows(li, pl.multiple_of(b * BB, BB))
                    return cc
                lax.fori_loop(0, ROWS // BB, rows2, 0)

            @pl.when(li < LAYERS - 1)
            def _():
                h_copy(li + 1).start()

            @pl.when(li == LAYERS)
            def _():
                pltpu.make_async_copy(g_v, og_hbm, g_sem).start()

        gather_step(k)

        @pl.when(k < 0)
        def _():
            @pl.when(t == 0)
            def _():
                h_copy(0).wait()
                g_copy().wait()
            for j in range(ROWS // BB // LEAD):
                prepare_rows(0, pl.multiple_of((t * (ROWS // BB // LEAD) + j) * BB, BB))

        @pl.when((k >= 0) & (k < NK))
        def _():
            row_phase(k)

        reduce_step(k)

        @pl.when((k >= 0) & (k < NK))
        def _():
            grad_phase(k)
        return carry

    lax.fori_loop(0, LEAD + NK + TAIL, step, 0)
    for m in range(3):
        out_copy(m, NK - 1).wait()
    pltpu.make_async_copy(g_v, og_hbm, g_sem).wait()


def fused(h, g, w1, w3, w2):
    any_spec = pl.BlockSpec(memory_space=pl.ANY)
    V = pltpu.VMEM
    wide, low = (DS, CH), (CPD, D)
    three = lambda *lead: [V(lead + wide, F32), V(lead + wide, F32), V(lead + low, F32)]
    scratch = [
        V((ROWS, D), BF), V((D, ROWS), BF), V((ROWS, D), BF), V((D, ROWS), BF),
        V((ROWS, D), F32), V((2, ROWS, D), BF), V((ROWS, CH), BF), V((ROWS, 2 * CH), BF),
        V((WS, 2, 2, 2, 2, 2 * DS, HALF), BF), V((WS, 2, 2, 2, 2, 2 * DS, HALF), BF), V((WS, 2, 2, 2, 2, CPD, D), BF),
        *three(2, 2, 2, 2, 2),
        *three(2, 2, 2, 2), *three(2, 2, 2), *three(2, 2), *three(2),
        *three(2, 2), *three(2), *three(),
        pltpu.SemaphoreType.DMA((3, 4, 2)), pltpu.SemaphoreType.DMA((3, 4, 2)),
        pltpu.SemaphoreType.DMA((3, 4, 2)), pltpu.SemaphoreType.DMA((3, 4, 2)),
        pltpu.SemaphoreType.DMA((3,)), pltpu.SemaphoreType.DMA((3,)),
        pltpu.SemaphoreType.DMA((2,)), pltpu.SemaphoreType.DMA(()),
    ]
    return pl.pallas_call(
        kernel,
        name='mlp_backward',
        out_shape=(
            jax.ShapeDtypeStruct((LAYERS, NC, DS, CH), F32),
            jax.ShapeDtypeStruct((LAYERS, NC, DS, CH), F32),
            jax.ShapeDtypeStruct((LAYERS, FS, D), F32),
            jax.ShapeDtypeStruct((ROWS, D), BF),
        ),
        in_specs=[any_spec] * 5,
        out_specs=(any_spec,) * 4,
        scratch_shapes=scratch,
        compiler_params=pltpu.CompilerParams(collective_id=0, has_side_effects=True, vmem_limit_bytes=67_043_328),
    )(h, g, w1, w3, w2)


def chunk_columns(w):
    w = w.reshape(LAYERS, DS, DEV, NC, CPD).transpose(0, 3, 1, 2, 4).reshape(LAYERS, NC, DS, CH)
    c = lax.axis_index('fsdp') % 2
    first = c == 0
    mine = jnp.where(first, w[..., :HALF], w[..., HALF:])
    sent = jnp.where(first, w[..., HALF:], w[..., :HALF])
    got = lax.ppermute(sent, 'fsdp', [(p, p ^ 1) for p in range(DEV)])
    return jnp.concatenate([jnp.where(first, mine, got), jnp.where(first, got, mine)], axis=2)


def restore_columns(o):
    return o.reshape(LAYERS, NC, DS, DEV, CPD).transpose(0, 2, 3, 1, 4).reshape(LAYERS, DS, FF)


def solution(mesh):
    weight_spec = P(None, 'fsdp', None)
    row_spec = P('fsdp', None)

    def local(h_saved, g_out, w_gate, w_up, w_down):
        o1, o3, o2, g = fused(h_saved, g_out, chunk_columns(w_gate), chunk_columns(w_up), w_down)
        return restore_columns(o1), restore_columns(o3), o2, g

    return jax.shard_map(local, mesh=mesh, in_specs=(weight_spec, row_spec, weight_spec, weight_spec, weight_spec), out_specs=(weight_spec, weight_spec, weight_spec, row_spec), check_vma=False)
```

time: 2160 us -> 843 us (0.39)
  waiting for transfers between devices: 1310 us -> 0.38 us
  Pallas kernels: 0 us -> 767 us
  matrix products: 742 us -> 0 us
  other arithmetic: 42.1 us -> 6.54 us
    reduce_scatter x9 -> x0, waiting for transfers between devices: 1230 us -> none  [the longest x3 549 us: local_backward(): lax.psum_scatter(grad_gate, 'fsdp', scatter_dimension=0, tiled=True)]
    pallas_call x0 -> x1, Pallas kernels: none -> 767 us  [fused(): pl.pallas_call(kernel, name='mlp_backward', out_shape=(jax.ShapeDtypeStru...]
    dot_general x24 -> x0, matrix products: 742 us -> none  [contract(): lax.dot_general(lhs, rhs, (((lhs_dim,), (rhs_dim,)), ((), ())), preferred...]
    all_gather x9 -> x0, waiting for transfers between devices: 74.2 us -> none  [the longest x3 28.5 us: local_backward(): gate_full = lax.all_gather(w_gate[layer_idx], 'fsdp', axis=0, tiled=True)]
    convert_element_type x3 -> x0, other arithmetic: 21.9 us -> none  [block_backward(): g_next = (g_rows.astype(jnp.float32) + d_resid).astype(jnp.bfloat16)]
  transfers between devices with their start and end apart: 18 -> 2, of which waited for: 10 -> 1; matrix products, arithmetic and copies ran while one was open for 38% -> 2% of each run, Pallas kernels for 0% -> 0%
where the time goes in v1:
time: 843 us
  Pallas kernels  767 us (91%)
  local copies, waits for them, and re-layouts  67 us (8%)
    pallas_call x1, Pallas kernels, fused(): pl.pallas_call(kernel, name='mlp_backward', out_shape=(jax.ShapeDtypeStru...  767 us
    unnamed x22, local copies, waits for them, and re-layouts  33.6 us
  transfers between devices with their start and end apart: 2, of which 1 were waited for; matrix products, arithmetic and copies ran while one was open for 2% of the time, Pallas kernels for 0%

profile of v1, /device:TPU:0, one launch (start us, length us, event | category | flops | bytes accessed | tf_op | source)
XLA Modules:
  0.0 842.8 jit_solution(12740373588479766980)
XLA Ops:
  0.6 4.5 copy.13
  5.2 3.1 copy.14
  8.3 1.5 fusion.1
  9.8 2.2 copy.27
  11.9 1.5 copy.28
  13.4 0.0 copy-start.5
  13.4 1.1 broadcast_select_fusion.6
  14.5 0.7 collective-permute-start
  15.3 0.0 copy-done.5
  15.3 3.1 copy.17
  18.3 3.1 copy.18
  21.4 1.5 fusion
  22.9 2.6 copy.29
  25.5 1.9 copy.30
  27.4 0.0 copy-start
  27.4 0.0 copy-start.1
  27.4 1.5 broadcast_select_fusion.2
  28.9 0.6 collective-permute-start.1
  29.6 0.0 collective-permute-done
  29.6 1.6 broadcast_select_fusion.5
  31.1 0.4 collective-permute-done.1
  31.5 0.0 copy-done
  31.5 0.0 copy-done.1
  31.5 0.4 broadcast_select_fusion.1
  32.0 2.0 pad_maximum_fusion
  33.9 766.8 %mlp_backward.1 = (f32[3,19,56,256]{3,2,1,0:T(8,128)}, f32[3,19,56,256]{3,2,1,0:T(8,128)}, f32[3,304,896]{2,1,0:T(8,128)}, bf16[2048,896]{1,0:T(8,128)(2,1)}) custom-call(bf16[3,2048,896]{2,1,0:T(8,128)(2,1)} %h_hbm.1, bf16[2048,896]{1,0:T(8,128)(2,1)} %g_hbm.1, bf16[3,19,112,128]{3,2,1,0:T(8,128)(2,1)} %get-tuple-element.24.w1_hbm, ...), custom_call_target="tpu_custom_call" | custom-call | tf_op jit(solution)/shard_map/mlp_backward/pallas_call | solution.py:344
  800.7 6.3 copy.21
  807.0 6.7 copy.22
  813.7 0.0 copy-start.4
  813.7 6.4 copy.25
  820.1 0.0 copy-done.4
  820.2 4.5 copy.23
  824.7 6.7 copy.24
  831.4 0.0 copy-start.3
  831.4 6.4 copy.26
  837.8 0.0 copy-done.3
  837.8 0.0 copy-start.2
  837.8 1.7 copy.33
  839.5 1.5 copy-done.2
  841.0 1.8 copy.34
Async XLA Ops:
  13.4 1.9 copy-start.5
  14.5 15.0 %collective-permute-start = (bf16[3,19,56,128]{3,2,1,0:T(8,128)(2,1)}, bf16[3,19,56,128]{3,2,1,0:T(8,128)(2,1)}, u32[]{:S(2)}, u32[]{:S(2)}) collective-permute-start(bf16[3,19,56,128]{3,2,1,0:T(8,128)(2,1)} %broadcast_select_fusion.6), channel_id=1, source_target_pairs={{0,1},{1,0},{2,3},{3,2},{4,5},{5,4},{6,7},{7,6},{8,9},{9,8},{10,11... | collective-permute-start | bytes 2451464 | tf_op jit(solution)/shard_map/ppermute | solution.py:366
  27.4 4.1 copy-start
  27.4 4.1 copy-start.1
  28.9 2.6 collective-permute-start.1
  813.7 6.4 copy-start.4
  831.4 6.4 copy-start.3
  837.8 3.2 copy-start.2

commit v2 on v1

--- a/solution.py
+++ b/solution.py
@@ -17,12 +17,14 @@
 CH = CPD * DEV
 NC = FF // CH
 NK = NC * LAYERS
-LEAD = 4
-TAIL = 5
+LEAD = 5
+TAIL = 4
 WS = 6
 RB = 1024
 BB = 256
 HALF = CH // 2
+LANES = 128
+NB = ROWS // BB
 MESH = pl.DeviceIdType.MESH
 BF = jnp.bfloat16
 F32 = jnp.float32
@@ -35,11 +37,12 @@
 def kernel(h_hbm, g_hbm, w1_hbm, w3_hbm, w2_hbm,
            o1_hbm, o3_hbm, o2_hbm, og_hbm,
            n_v, nt_v, g_v, gt_v, dn_v, h_v, a_v, d_v,
+           c1_v, c3_v, e1_v, e3_v, f1_v, f3_v, t1_v, t3_v,
            w1_v, w3_v, w2_v,
            g1_v, g3_v, g2_v,
            rd1, rd3, rd2, ra1, ra3, ra2, rb1, rb3, rb2, rc1, rc3, rc2,
-           pa1, pa3, pa2, pb1, pb3, pb2, s1, s3, s2,
-           ag_send, ag_recv, rs_send, rs_recv, own_sem, out_sem, h_sem, g_sem):
+           pa1, pa3, pa2, pb1, pb3, pb2, s2,
+           ag_send, ag_recv, rs_send, rs_recv, ex_send, ex_recv, own_sem, out_sem, cols_sem, h_sem, g_sem):
     me = lax.axis_index('fsdp')
     c = me % 2
     x = (me // 2) % 2
@@ -58,7 +61,8 @@
     weights = (w1_v, w3_v, w2_v)
     grads = (g1_v, g3_v, g2_v)
     rds, ras, rbs, rcs = (rd1, rd3, rd2), (ra1, ra3, ra2), (rb1, rb3, rb2), (rc1, rc3, rc2)
-    pas, pbs, outs = (pa1, pa3, pa2), (pb1, pb3, pb2), (s1, s3, s2)
+    pas, pbs, outs = (pa1, pa3, pa2), (pb1, pb3, pb2), (t1_v, t3_v, s2)
+    cols, halves, theirs = (c1_v, c3_v), (e1_v, e3_v), (f1_v, f3_v)
     order = ((nx, ny, nz), (ny, nz, nx), (nz, nx, ny))
 
     def gather_slice(m, stage, k):
@@ -70,24 +74,66 @@
             return (w.at[s, c, z, y, x], w.at[s, c, z, :, x], w.at[s, c, :, :, x], w.at[s, c])[stage]
         return (w.at[s, z, y, x, c], w.at[s, :, y, x, c], w.at[s, :, y, :, c], w.at[s, :, :, :, c])[stage]
 
-    def own_block(m, k):
-        layer = LAYERS - 1 - k // NC
-        i = lax.rem(k, NC)
-        if m == 2:
-            return w2_hbm.at[layer, pl.ds(pl.multiple_of(i * CPD, CPD), CPD)]
-        return (w1_hbm, w3_hbm)[m].at[layer, i]
+    def own_rows(k):
+        return w2_hbm.at[LAYERS - 1 - k // NC, pl.ds(pl.multiple_of(lax.rem(k, NC) * CPD, CPD), CPD)]
 
     def gather_copy(m, stage, k):
         par = lax.rem(k, 2)
         dst = gather_slice(m, stage, k)
-        src = own_block(m, k) if stage == 0 else dst
+        src = own_rows(k) if (stage == 0 and m == 2) else dst
         peer = core if stage == 3 else order[m][stage]
         return pltpu.make_async_remote_copy(
             src_ref=src, dst_ref=dst, send_sem=ag_send.at[m, stage, par], recv_sem=ag_recv.at[m, stage, par],
             device_id=(peer,), device_id_type=MESH)
 
-    def own_copy(m, k):
-        return pltpu.make_async_copy(own_block(m, k), gather_slice(m, 0, k), own_sem.at[m])
+    def own_copy(k):
+        return pltpu.make_async_copy(own_rows(k), gather_slice(2, 0, k), own_sem)
+
+    def cols_copy(m, li):
+        slot = lax.rem(li, 2)
+        return pltpu.make_async_copy((w1_hbm, w3_hbm)[m].at[LAYERS - 1 - li], cols[m].at[slot], cols_sem.at[m, slot])
+
+    def half_copy(m, k):
+        par = lax.rem(k, 2)
+        return pltpu.make_async_remote_copy(
+            src_ref=halves[m].at[1 - c], dst_ref=theirs[m].at[par], send_sem=ex_send.at[m, par], recv_sem=ex_recv.at[m, par],
+            device_id=(core,), device_id_type=MESH)
+
+    lane = lax.broadcasted_iota(jnp.int32, (DS, LANES), 1)
+
+    def place(p, i):
+        col = FS * p + CPD * i
+        tile = col // LANES
+        return pl.ds(pl.multiple_of(tile * LANES, LANES), LANES), col - tile * LANES
+
+    def pick_columns(k):
+        li = k // NC
+        i = lax.rem(k, NC)
+        slot = lax.rem(li, 2)
+        for m in range(2):
+            for half in range(2):
+                acc = jnp.zeros((DS, LANES), F32)
+                for q in range(DEV // 2):
+                    tile, off = place(half * (DEV // 2) + q, i)
+                    part = pltpu.roll(cols[m][slot, :, tile].astype(F32), lax.rem(CPD * q + LANES - off, LANES), 1)
+                    acc = jnp.where((lane >= CPD * q) & (lane < CPD * (q + 1)), part, acc)
+                halves[m][half] = acc
+
+    def merge_rows(k):
+        par = lax.rem(k, 2)
+        for m in range(2):
+            mine, other = halves[m][c], theirs[m][par]
+            low = jnp.where(c == 0, mine, other)
+            high = jnp.where(c == 0, other, mine)
+            weights[m][lax.rem(k, WS), c, z, y, x] = jnp.concatenate([low, high], axis=0).astype(BF)
+
+    def put_columns(m, i, value):
+        for half in range(2):
+            src = value[:, half * LANES:(half + 1) * LANES]
+            for q in range(DEV // 2):
+                tile, off = place(half * (DEV // 2) + q, i)
+                part = pltpu.roll(src, lax.rem(off + LANES - CPD * q, LANES), 1)
+                outs[m][:, tile] = jnp.where((lane >= off) & (lane < off + CPD), part, outs[m][:, tile])
 
     def reduce_copy(m, stage, k):
         par = lax.rem(k, 2)
@@ -109,31 +155,31 @@
 
     def out_copy(m, k):
         layer = LAYERS - 1 - k // NC
-        i = lax.rem(k, NC)
         if m == 2:
-            dst = o2_hbm.at[layer, pl.ds(pl.multiple_of(i * CPD, CPD), CPD)]
+            dst = o2_hbm.at[layer, pl.ds(pl.multiple_of(lax.rem(k, NC) * CPD, CPD), CPD)]
         else:
-            dst = (o1_hbm, o3_hbm)[m].at[layer, i]
+            dst = (o1_hbm, o3_hbm)[m].at[layer]
         return pltpu.make_async_copy(outs[m], dst, out_sem.at[m])
 
-    def h_copy(li):
-        return pltpu.make_async_copy(h_hbm.at[LAYERS - 1 - li], h_v.at[lax.rem(li, 2)], h_sem.at[lax.rem(li, 2)])
+    def h_copy(li, b):
+        rows = pl.ds(pl.multiple_of(b * BB, BB), BB)
+        return pltpu.make_async_copy(h_hbm.at[LAYERS - 1 - li, rows], h_v.at[rows], h_sem.at[b])
 
     def g_copy():
         return pltpu.make_async_copy(g_hbm, g_v, g_sem)
 
-    def finalize_rows(li, r0):
+    def finalize_rows(r0):
         rows = pl.ds(r0, BB)
-        hf = h_v[lax.rem(li, 2), rows, :].astype(F32)
+        hf = h_v[rows, :].astype(F32)
         r = lax.rsqrt(jnp.mean(hf * hf, axis=-1, keepdims=True) + EPS)
         m = hf * r
         dn = dn_v[rows, :]
         dr = r * (dn - m * jnp.mean(dn * m, axis=-1, keepdims=True))
         g_v[rows, :] = (g_v[rows, :].astype(F32) + dr).astype(BF)
 
-    def prepare_rows(li, r0):
+    def prepare_rows(r0):
         rows = pl.ds(r0, BB)
-        hf = h_v[lax.rem(li, 2), rows, :].astype(F32)
+        hf = h_v[rows, :].astype(F32)
         r = lax.rsqrt(jnp.mean(hf * hf, axis=-1, keepdims=True) + EPS)
         nb = (hf * r).astype(BF)
         n_v[rows, :] = nb
@@ -152,40 +198,78 @@
             def _():
                 for m in range(3):
                     gather_copy(m, stage, k + lag).wait()
-                    if stage == 0:
-                        own_copy(m, k + lag).wait()
+                if stage == 0:
+                    own_copy(k + lag).wait()
 
         for lag, stage in ((1, 3), (2, 2), (3, 1), (4, 0)):
             @pl.when((k + lag >= 0) & (k + lag < NK))
             def _():
                 for m in range(3):
                     gather_copy(m, stage, k + lag).start()
-                    if stage == 0:
-                        own_copy(m, k + lag).start()
+                if stage == 0:
+                    own_copy(k + lag).start()
 
         @pl.when((k >= 1) & (k <= NK))
         def _():
             for m in range(3):
                 reduce_copy(m, 0, k - 1).start()
+
+        @pl.when(k + 5 < NK)
+        def _():
+            kn = k + 5
+            li = kn // NC
+
+            @pl.when(lax.rem(kn, NC) == 0)
+            def _():
+                for m in range(2):
+                    cols_copy(m, li).wait()
+            pick_columns(kn)
+            for m in range(2):
+                half_copy(m, kn).start()
+
+            @pl.when((lax.rem(kn, NC) == NC - 1) & (li == 0))
+            def _():
+                for m in range(2):
+                    cols_copy(m, 2).start()
 
     def reduce_step(k):
         def live(lag):
             return (k - lag >= 0) & (k - lag < NK)
 
+        @pl.when(k + 5 < NK)
+        def _():
+            for m in range(2):
+                half_copy(m, k + 5).wait()
+            merge_rows(k + 5)
+
         @pl.when(live(4))
         def _():
             kf = k - 4
             par = lax.rem(kf, 2)
 
+            i = lax.rem(kf, NC)
+
             @pl.when(kf >= 1)
             def _():
-                for m in range(3):
+                out_copy(2, kf - 1).wait()
+
+            @pl.when((kf >= 1) & (i == 0))
+            def _():
+                for m in range(2):
                     out_copy(m, kf - 1).wait()
             for m in range(3):
                 reduce_copy(m, 3, kf).wait()
-                keep = (z, x, y)[m]
-                outs[m][...] = rcs[m][par] + pbs[m][keep]
-                out_copy(m, kf).start()
+                done = rcs[m][par] + pbs[m][(z, x, y)[m]]
+                if m == 2:
+                    s2[...] = done
+                else:
+                    put_columns(m, i, done)
+            out_copy(2, kf).start()
+
+            @pl.when(i == NC - 1)
+            def _():
+                for m in range(2):
+                    out_copy(m, kf).start()
 
         @pl.when(live(3))
         def _():
@@ -259,63 +343,67 @@
         g3_v[par] = dot(nt, d_v[:, pl.ds(CH, CH)], 1, 0).reshape(2, 2, 2, 2, DS, CH)
         g2_v[par] = dot(gt_v[...], a_v[...], 1, 0).T.reshape(2, 2, 2, 2, CPD, D)
 
-    h_copy(0).start()
+    for m in range(2):
+        cols_copy(m, 0).start()
+    for b in range(NB):
+        h_copy(0, b).start()
     g_copy().start()
-    h_copy(1).start()
+    for m in range(2):
+        cols_copy(m, 1).start()
 
     def step(t, carry):
         k = t - LEAD
-
-        @pl.when(t == 0)
-        def _():
-            pass
-
-        @pl.when((k == NC) | (k == 2 * NC) | (k == NK))
+        inside = (k >= 0) & (k < NK)
+        last = inside & (lax.rem(k + NC, NC) == NC - 1)
+        gather_step(k)
+
+        @pl.when((t >= 1) & (t < LEAD))
+        def _():
+            @pl.when(t == 1)
+            def _():
+                for b in range(NB):
+                    h_copy(0, b).wait()
+                g_copy().wait()
+            per = NB // (LEAD - 1)
+            for j in range(per):
+                prepare_rows(pl.multiple_of(((t - 1) * per + j) * BB, BB))
+
+        @pl.when(inside)
+        def _():
+            row_phase(k)
+
+        @pl.when(last)
         def _():
             li = k // NC
 
             def rows(b, cc):
-                finalize_rows(li - 1, pl.multiple_of(b * BB, BB))
+                finalize_rows(pl.multiple_of(b * BB, BB))
+
+                @pl.when(li < LAYERS - 1)
+                def _():
+                    h_copy(li + 1, b).start()
                 return cc
-            lax.fori_loop(0, ROWS // BB, rows, 0)
-
-            @pl.when(li < LAYERS)
-            def _():
-                h_copy(li).wait()
-
-                def rows2(b, cc):
-                    prepare_rows(li, pl.multiple_of(b * BB, BB))
-                    return cc
-                lax.fori_loop(0, ROWS // BB, rows2, 0)
-
-            @pl.when(li < LAYERS - 1)
-            def _():
-                h_copy(li + 1).start()
-
-            @pl.when(li == LAYERS)
+            lax.fori_loop(0, NB, rows, 0)
+
+            @pl.when(li == LAYERS - 1)
             def _():
                 pltpu.make_async_copy(g_v, og_hbm, g_sem).start()
 
-        gather_step(k)
-
-        @pl.when(k < 0)
-        def _():
-            @pl.when(t == 0)
-            def _():
-                h_copy(0).wait()
-                g_copy().wait()
-            for j in range(ROWS // BB // LEAD):
-                prepare_rows(0, pl.multiple_of((t * (ROWS // BB // LEAD) + j) * BB, BB))
-
-        @pl.when((k >= 0) & (k < NK))
-        def _():
-            row_phase(k)
-
         reduce_step(k)
 
-        @pl.when((k >= 0) & (k < NK))
+        @pl.when(inside)
         def _():
             grad_phase(k)
+
+        @pl.when(last & (k < NK - 1))
+        def _():
+            li = k // NC
+
+            def rows(b, cc):
+                h_copy(li + 1, b).wait()
+                prepare_rows(pl.multiple_of(b * BB, BB))
+                return cc
+            lax.fori_loop(0, NB, rows, 0)
         return carry
 
     lax.fori_loop(0, LEAD + NK + TAIL, step, 0)
@@ -331,22 +419,25 @@
     three = lambda *lead: [V(lead + wide, F32), V(lead + wide, F32), V(lead + low, F32)]
     scratch = [
         V((ROWS, D), BF), V((D, ROWS), BF), V((ROWS, D), BF), V((D, ROWS), BF),
-        V((ROWS, D), F32), V((2, ROWS, D), BF), V((ROWS, CH), BF), V((ROWS, 2 * CH), BF),
+        V((ROWS, D), F32), V((ROWS, D), BF), V((ROWS, CH), BF), V((ROWS, 2 * CH), BF),
+        V((2, DS, FF), BF), V((2, DS, FF), BF), V((2, DS, LANES), F32), V((2, DS, LANES), F32),
+        V((2, DS, LANES), F32), V((2, DS, LANES), F32), V((DS, FF), F32), V((DS, FF), F32),
         V((WS, 2, 2, 2, 2, 2 * DS, HALF), BF), V((WS, 2, 2, 2, 2, 2 * DS, HALF), BF), V((WS, 2, 2, 2, 2, CPD, D), BF),
         *three(2, 2, 2, 2, 2),
         *three(2, 2, 2, 2), *three(2, 2, 2), *three(2, 2), *three(2),
-        *three(2, 2), *three(2), *three(),
+        *three(2, 2), *three(2), V(low, F32),
         pltpu.SemaphoreType.DMA((3, 4, 2)), pltpu.SemaphoreType.DMA((3, 4, 2)),
         pltpu.SemaphoreType.DMA((3, 4, 2)), pltpu.SemaphoreType.DMA((3, 4, 2)),
-        pltpu.SemaphoreType.DMA((3,)), pltpu.SemaphoreType.DMA((3,)),
-        pltpu.SemaphoreType.DMA((2,)), pltpu.SemaphoreType.DMA(()),
+        pltpu.SemaphoreType.DMA((2, 2)), pltpu.SemaphoreType.DMA((2, 2)),
+        pltpu.SemaphoreType.DMA(()), pltpu.SemaphoreType.DMA((3,)), pltpu.SemaphoreType.DMA((2, 2)),
+        pltpu.SemaphoreType.DMA((NB,)), pltpu.SemaphoreType.DMA(()),
     ]
     return pl.pallas_call(
         kernel,
         name='mlp_backward',
         out_shape=(
-            jax.ShapeDtypeStruct((LAYERS, NC, DS, CH), F32),
-            jax.ShapeDtypeStruct((LAYERS, NC, DS, CH), F32),
+            jax.ShapeDtypeStruct((LAYERS, DS, FF), F32),
+            jax.ShapeDtypeStruct((LAYERS, DS, FF), F32),
             jax.ShapeDtypeStruct((LAYERS, FS, D), F32),
             jax.ShapeDtypeStruct((ROWS, D), BF),
         ),
@@ -357,26 +448,8 @@
     )(h, g, w1, w3, w2)
 
 
-def chunk_columns(w):
-    w = w.reshape(LAYERS, DS, DEV, NC, CPD).transpose(0, 3, 1, 2, 4).reshape(LAYERS, NC, DS, CH)
-    c = lax.axis_index('fsdp') % 2
-    first = c == 0
-    mine = jnp.where(first, w[..., :HALF], w[..., HALF:])
-    sent = jnp.where(first, w[..., HALF:], w[..., :HALF])
-    got = lax.ppermute(sent, 'fsdp', [(p, p ^ 1) for p in range(DEV)])
-    return jnp.concatenate([jnp.where(first, mine, got), jnp.where(first, got, mine)], axis=2)
-
-
-def restore_columns(o):
-    return o.reshape(LAYERS, NC, DS, DEV, CPD).transpose(0, 2, 3, 1, 4).reshape(LAYERS, DS, FF)
-
-
 def solution(mesh):
     weight_spec = P(None, 'fsdp', None)
     row_spec = P('fsdp', None)
 
-    def local(h_saved, g_out, w_gate, w_up, w_down):
-        o1, o3, o2, g = fused(h_saved, g_out, chunk_columns(w_gate), chunk_columns(w_up), w_down)
-        return restore_columns(o1), restore_columns(o3), o2, g
-
-    return jax.shard_map(local, mesh=mesh, in_specs=(weight_spec, row_spec, weight_spec, weight_spec, weight_spec), out_specs=(weight_spec, weight_spec, weight_spec, row_spec), check_vma=False)
+    return jax.shard_map(fused, mesh=mesh, in_specs=(weight_spec, row_spec, weight_spec, weight_spec, weight_spec), out_specs=(weight_spec, weight_spec, weight_spec, row_spec), check_vma=False)

time: 843 us -> 783 us (0.929)
  local copies, waits for them, and re-layouts: 67 us -> 12.2 us
    unnamed x22 -> x10, local copies, waits for them, and re-layouts: 33.6 us -> 12.2 us
    transpose x4 -> x0, local copies, waits for them, and re-layouts: 19.5 us -> none  [the longest x2 13.4 us: restore_columns(): o.reshape(LAYERS, NC, DS, DEV, CPD).transpose(0, 2, 3, 1, 4)]
    pallas_call x2 -> x0, local copies, waits for them, and re-layouts: 10.8 us -> none  [fused(): pl.pallas_call(kernel, name='mlp_backward', out_shape=(jax.ShapeDtypeStru...]
  transfers between devices with their start and end apart: 2 -> 0, of which waited for: 1 -> 0; matrix products, arithmetic and copies ran while one was open for 2% -> 0% of each run, Pallas kernels for 0% -> 0%
where the time goes in v2:
time: 783 us
  Pallas kernels  770 us (98%)
  local copies, waits for them, and re-layouts  12.2 us (2%)
    pallas_call x1, Pallas kernels, fused(): pl.pallas_call(kernel, name='mlp_backward', out_shape=(jax.ShapeDtypeStru...  770 us

profile of v2, /device:TPU:0, one launch (start us, length us, event | category | flops | bytes accessed | tf_op | source)
XLA Modules:
  0.0 783.1 jit_solution(943016263544751627)
XLA Ops:
  0.6 770.3 %mlp_backward.1 = (f32[3,56,4864]{2,1,0:T(8,128)}, f32[3,56,4864]{2,1,0:T(8,128)}, f32[3,304,896]{2,1,0:T(8,128)}, bf16[2048,896]{1,0:T(8,128)(2,1)}) custom-call(bf16[3,2048,896]{2,1,0:T(8,128)(2,1)} %h_hbm.1, bf16[2048,896]{1,0:T(8,128)(2,1)} %g_hbm.1, bf16[3,56,4864]{2,1,0:T(8,128)(2,1)} %w1_hbm.1, bf16[3,56,4864]{2,1,0:T(8,128)(2,1)} %w3_hbm.1, ...), custom_call_target="tpu_custom_call" | custom-call | tf_op jit(solution)/shard_map/mlp_backward/pallas_call | solution.py:435
  770.9 0.0 copy-start.2
  770.9 4.0 copy.13
  774.9 0.0 copy-done.2
  774.9 0.0 copy-start.1
  774.9 1.7 copy.14
  776.6 1.4 copy-done.1
  778.0 0.0 copy-start
  778.0 1.7 copy.15
  779.7 1.5 copy-done
  781.2 1.8 copy.16
Async XLA Ops:
  770.9 4.0 copy-start.2
  774.9 3.1 copy-start.1
  778.0 3.2 copy-start

commit v3 on v2

--- a/solution.py
+++ b/solution.py
@@ -41,7 +41,7 @@
            w1_v, w3_v, w2_v,
            g1_v, g3_v, g2_v,
            rd1, rd3, rd2, ra1, ra3, ra2, rb1, rb3, rb2, rc1, rc3, rc2,
-           pa1, pa3, pa2, pb1, pb3, pb2, s2,
+           pa1, pa3, pa2, pb1, pb3, pb2, s1, s3, s2,
            ag_send, ag_recv, rs_send, rs_recv, ex_send, ex_recv, own_sem, out_sem, cols_sem, h_sem, g_sem):
     me = lax.axis_index('fsdp')
     c = me % 2
@@ -56,12 +56,11 @@
     barrier = pltpu.get_barrier_semaphore()
     for peer in (core, nx, ny, nz):
         pl.semaphore_signal(barrier, inc=1, device_id=(peer,), device_id_type=MESH)
-    pl.semaphore_wait(barrier, 4)
-
     weights = (w1_v, w3_v, w2_v)
     grads = (g1_v, g3_v, g2_v)
     rds, ras, rbs, rcs = (rd1, rd3, rd2), (ra1, ra3, ra2), (rb1, rb3, rb2), (rc1, rc3, rc2)
     pas, pbs, outs = (pa1, pa3, pa2), (pb1, pb3, pb2), (t1_v, t3_v, s2)
+    dones = (s1, s3, s2)
     cols, halves, theirs = (c1_v, c3_v), (e1_v, e3_v), (f1_v, f3_v)
     order = ((nx, ny, nz), (ny, nz, nx), (nz, nx, ny))
 
@@ -127,9 +126,13 @@
             high = jnp.where(c == 0, other, mine)
             weights[m][lax.rem(k, WS), c, z, y, x] = jnp.concatenate([low, high], axis=0).astype(BF)
 
-    def put_columns(m, i, value):
+    def put_columns(i):
+        for m in range(2):
+            put_matrix(m, i)
+
+    def put_matrix(m, i):
         for half in range(2):
-            src = value[:, half * LANES:(half + 1) * LANES]
+            src = dones[m][:, half * LANES:(half + 1) * LANES]
             for q in range(DEV // 2):
                 tile, off = place(half * (DEV // 2) + q, i)
                 part = pltpu.roll(src, lax.rem(off + LANES - CPD * q, LANES), 1)
@@ -137,7 +140,8 @@
 
     def reduce_copy(m, stage, k):
         par = lax.rem(k, 2)
-        g, pa, pb = grads[m], pas[m], pbs[m]
+        slot = lax.rem(k, 3) if stage == 3 else par
+        g, pa, pb = grads[m], pas[m].at[par], pbs[m].at[par]
         if stage == 0:
             src, dst, peer = g.at[par, :, :, :, 1 - c], rds[m].at[par], core
         elif stage == 1:
@@ -148,9 +152,9 @@
             dst, peer = rbs[m].at[par], order[m][1]
         else:
             src = (pb.at[1 - z], pb.at[1 - x], pb.at[1 - y])[m]
-            dst, peer = rcs[m].at[par], order[m][2]
+            dst, peer = rcs[m].at[lax.rem(k, 3)], order[m][2]
         return pltpu.make_async_remote_copy(
-            src_ref=src, dst_ref=dst, send_sem=rs_send.at[m, stage, par], recv_sem=rs_recv.at[m, stage, par],
+            src_ref=src, dst_ref=dst, send_sem=rs_send.at[m, stage, slot], recv_sem=rs_recv.at[m, stage, slot],
             device_id=(peer,), device_id_type=MESH)
 
     def out_copy(m, k):
@@ -188,6 +192,11 @@
         dn_v[rows, :] = jnp.zeros((BB, D), F32)
 
     def gather_step(k):
+        @pl.when((k >= 1) & (k <= NK))
+        def _():
+            for m in range(3):
+                reduce_copy(m, 0, k - 1).start()
+
         @pl.when((k >= 0) & (k < NK))
         def _():
             for m in range(3):
@@ -209,44 +218,31 @@
                 if stage == 0:
                     own_copy(k + lag).start()
 
-        @pl.when((k >= 1) & (k <= NK))
-        def _():
-            for m in range(3):
-                reduce_copy(m, 0, k - 1).start()
+        @pl.when((k <= 0) & (k > -LEAD))
+        def _():
+            pick_columns(k + 5)
 
         @pl.when(k + 5 < NK)
         def _():
-            kn = k + 5
-            li = kn // NC
-
-            @pl.when(lax.rem(kn, NC) == 0)
-            def _():
-                for m in range(2):
-                    cols_copy(m, li).wait()
-            pick_columns(kn)
             for m in range(2):
-                half_copy(m, kn).start()
-
-            @pl.when((lax.rem(kn, NC) == NC - 1) & (li == 0))
-            def _():
-                for m in range(2):
-                    cols_copy(m, 2).start()
+                half_copy(m, k + 5).start()
+
+        @pl.when(k + 5 == NC - 1)
+        def _():
+            for m in range(2):
+                cols_copy(m, 2).start()
+
+        @pl.when((k + 6 == NC) | (k + 6 == 2 * NC))
+        def _():
+            for m in range(2):
+                cols_copy(m, (k + 6) // NC).wait()
 
     def reduce_step(k):
         def live(lag):
             return (k - lag >= 0) & (k - lag < NK)
 
-        @pl.when(k + 5 < NK)
-        def _():
-            for m in range(2):
-                half_copy(m, k + 5).wait()
-            merge_rows(k + 5)
-
-        @pl.when(live(4))
-        def _():
+        def finish():
             kf = k - 4
-            par = lax.rem(kf, 2)
-
             i = lax.rem(kf, NC)
 
             @pl.when(kf >= 1)
@@ -259,55 +255,66 @@
                     out_copy(m, kf - 1).wait()
             for m in range(3):
                 reduce_copy(m, 3, kf).wait()
-                done = rcs[m][par] + pbs[m][(z, x, y)[m]]
-                if m == 2:
-                    s2[...] = done
-                else:
-                    put_columns(m, i, done)
+            for m in range(3):
+                dones[m][...] = rcs[m][lax.rem(kf, 3)] + pbs[m][lax.rem(kf, 2), (z, x, y)[m]]
             out_copy(2, kf).start()
 
-            @pl.when(i == NC - 1)
-            def _():
-                for m in range(2):
-                    out_copy(m, kf).start()
-
-        @pl.when(live(3))
-        def _():
+        def third():
             kf = k - 3
             par = lax.rem(kf, 2)
             for m in range(3):
                 reduce_copy(m, 2, kf).wait()
+            for m in range(3):
                 for a in range(2):
-                    kept = (lambda: pa1[a, y], lambda: pa3[z, a], lambda: pa2[a, x])[m]()
-                    pbs[m][a] = rbs[m][par, a] + kept
-
-        @pl.when(live(2))
-        def _():
+                    kept = (lambda: pa1[par, a, y], lambda: pa3[par, z, a], lambda: pa2[par, a, x])[m]()
+                    pbs[m][par, a] = rbs[m][par, a] + kept
+            for m in range(3):
+                reduce_copy(m, 3, kf).start()
+
+        def second():
             kf = k - 2
             par = lax.rem(kf, 2)
             for m in range(3):
                 reduce_copy(m, 1, kf).wait()
+            for m in range(3):
                 for a in range(2):
                     for b in range(2):
                         kept = (lambda: g1_v[par, a, b, x, c], lambda: g3_v[par, a, y, b, c], lambda: g2_v[par, z, a, b, c])[m]()
-                        pas[m][a, b] = ras[m][par, a, b] + kept
-
-        @pl.when(live(1))
-        def _():
+                        pas[m][par, a, b] = ras[m][par, a, b] + kept
+            for m in range(3):
+                reduce_copy(m, 2, kf).start()
+
+        def first():
             kf = k - 1
             par = lax.rem(kf, 2)
             for m in range(3):
                 reduce_copy(m, 0, kf).wait()
+            for m in range(3):
                 for a in range(2):
                     for b in range(2):
                         for d in range(2):
                             grads[m][par, a, b, d, c] = grads[m][par, a, b, d, c] + rds[m][par, a, b, d]
-
-        for lag, stage in ((3, 3), (2, 2), (1, 1)):
-            @pl.when(live(lag))
-            def _():
-                for m in range(3):
-                    reduce_copy(m, stage, k - lag).start()
+            for m in range(3):
+                reduce_copy(m, 1, kf).start()
+
+        @pl.when(k + 5 < NK)
+        def _():
+            for m in range(2):
+                half_copy(m, k + 5).wait()
+            merge_rows(k + 5)
+
+        @pl.when(k <= NK)
+        def _():
+            pl.when(live(4))(finish)
+            pl.when(live(3))(third)
+            pl.when(live(2))(second)
+            pl.when(live(1))(first)
+
+        @pl.when(k > NK)
+        def _():
+            pl.when(live(2))(second)
+            pl.when(live(3))(third)
+            pl.when(live(4))(finish)
 
     def row_phase(k):
         s = lax.rem(k, WS)
@@ -338,6 +345,8 @@
 
     def grad_phase(k):
         par = lax.rem(k, 2)
+        pick_columns(k + 6)
+        put_columns(lax.rem(k - 4 + NC, NC))
         nt = nt_v[...]
         g1_v[par] = dot(nt, d_v[:, pl.ds(0, CH)], 1, 0).reshape(2, 2, 2, 2, DS, CH)
         g3_v[par] = dot(nt, d_v[:, pl.ds(CH, CH)], 1, 0).reshape(2, 2, 2, 2, DS, CH)
@@ -350,6 +359,10 @@
     g_copy().start()
     for m in range(2):
         cols_copy(m, 1).start()
+    for m in range(2):
+        cols_copy(m, 0).wait()
+    pick_columns(0)
+    pl.semaphore_wait(barrier, 4)
 
     def step(t, carry):
         k = t - LEAD
@@ -372,20 +385,20 @@
         def _():
             row_phase(k)
 
-        @pl.when(last)
+        @pl.when((last & (k < NK - 1)) | (k == NK))
         def _():
             li = k // NC
 
             def rows(b, cc):
                 finalize_rows(pl.multiple_of(b * BB, BB))
 
-                @pl.when(li < LAYERS - 1)
+                @pl.when(k < NK)
                 def _():
                     h_copy(li + 1, b).start()
                 return cc
             lax.fori_loop(0, NB, rows, 0)
 
-            @pl.when(li == LAYERS - 1)
+            @pl.when(k == NK)
             def _():
                 pltpu.make_async_copy(g_v, og_hbm, g_sem).start()
 
@@ -394,6 +407,15 @@
         @pl.when(inside)
         def _():
             grad_phase(k)
+
+        @pl.when(k >= NK)
+        def _():
+            put_columns(lax.rem(k - 4, NC))
+
+        @pl.when((k >= 4) & (lax.rem(k - 4 + NC, NC) == NC - 1))
+        def _():
+            for m in range(2):
+                out_copy(m, k - 4).start()
 
         @pl.when(last & (k < NK - 1))
         def _():
@@ -410,6 +432,25 @@
     for m in range(3):
         out_copy(m, NK - 1).wait()
     pltpu.make_async_copy(g_v, og_hbm, g_sem).wait()
+
+
+def hand_out(*refs):
+    srcs, dsts, bufs, sem_in, sem_out = refs[:4], refs[4:8], refs[8:12], refs[12], refs[13]
+    pieces = []
+    for j in range(4):
+        if j < 3:
+            pieces += [(j, layer) for layer in range(LAYERS)]
+        else:
+            pieces += [(j, pl.ds(q * (ROWS // 4), ROWS // 4)) for q in range(4)]
+    ins = [pltpu.make_async_copy(srcs[j].at[w], bufs[j].at[w], sem_in.at[n]) for n, (j, w) in enumerate(pieces)]
+    outs = [pltpu.make_async_copy(bufs[j].at[w], dsts[j].at[w], sem_out.at[n]) for n, (j, w) in enumerate(pieces)]
+    for copy in ins:
+        copy.start()
+    for copy, out in zip(ins, outs):
+        copy.wait()
+        out.start()
+    for out in outs:
+        out.wait()
 
 
 def fused(h, g, w1, w3, w2):
@@ -424,28 +465,39 @@
         V((2, DS, LANES), F32), V((2, DS, LANES), F32), V((DS, FF), F32), V((DS, FF), F32),
         V((WS, 2, 2, 2, 2, 2 * DS, HALF), BF), V((WS, 2, 2, 2, 2, 2 * DS, HALF), BF), V((WS, 2, 2, 2, 2, CPD, D), BF),
         *three(2, 2, 2, 2, 2),
-        *three(2, 2, 2, 2), *three(2, 2, 2), *three(2, 2), *three(2),
-        *three(2, 2), *three(2), V(low, F32),
+        *three(2, 2, 2, 2), *three(2, 2, 2), *three(2, 2), *three(3),
+        *three(2, 2, 2), *three(2, 2), *three(),
         pltpu.SemaphoreType.DMA((3, 4, 2)), pltpu.SemaphoreType.DMA((3, 4, 2)),
-        pltpu.SemaphoreType.DMA((3, 4, 2)), pltpu.SemaphoreType.DMA((3, 4, 2)),
+        pltpu.SemaphoreType.DMA((3, 4, 3)), pltpu.SemaphoreType.DMA((3, 4, 3)),
         pltpu.SemaphoreType.DMA((2, 2)), pltpu.SemaphoreType.DMA((2, 2)),
         pltpu.SemaphoreType.DMA(()), pltpu.SemaphoreType.DMA((3,)), pltpu.SemaphoreType.DMA((2, 2)),
         pltpu.SemaphoreType.DMA((NB,)), pltpu.SemaphoreType.DMA(()),
     ]
-    return pl.pallas_call(
+    results = (
+        jax.ShapeDtypeStruct((LAYERS, DS, FF), F32),
+        jax.ShapeDtypeStruct((LAYERS, DS, FF), F32),
+        jax.ShapeDtypeStruct((LAYERS, FS, D), F32),
+        jax.ShapeDtypeStruct((ROWS, D), BF),
+    )
+    parts = pl.pallas_call(
         kernel,
         name='mlp_backward',
-        out_shape=(
-            jax.ShapeDtypeStruct((LAYERS, DS, FF), F32),
-            jax.ShapeDtypeStruct((LAYERS, DS, FF), F32),
-            jax.ShapeDtypeStruct((LAYERS, FS, D), F32),
-            jax.ShapeDtypeStruct((ROWS, D), BF),
-        ),
+        out_shape=results,
         in_specs=[any_spec] * 5,
         out_specs=(any_spec,) * 4,
         scratch_shapes=scratch,
         compiler_params=pltpu.CompilerParams(collective_id=0, has_side_effects=True, vmem_limit_bytes=67_043_328),
     )(h, g, w1, w3, w2)
+    return pl.pallas_call(
+        hand_out,
+        name='hand_out',
+        out_shape=results,
+        in_specs=[any_spec] * 4,
+        out_specs=(any_spec,) * 4,
+        scratch_shapes=[V(r.shape, r.dtype) for r in results] + [pltpu.SemaphoreType.DMA((13,)), pltpu.SemaphoreType.DMA((13,))],
+        compiler_params=pltpu.CompilerParams(vmem_limit_bytes=67_043_328),
+        cost_estimate=pl.CostEstimate(flops=0, bytes_accessed=27_000_000, transcendentals=0),
+    )(*parts)
 
 
 def solution(mesh):

time: 783 us -> 775 us (0.990)
  local copies, waits for them, and re-layouts: 12.2 us -> 0 us
    unnamed x10 -> x0, local copies, waits for them, and re-layouts: 12.2 us -> none
    pallas_call x1 -> x2, Pallas kernels: 770 us -> 774 us  [the longest x1 764 us: fused(): pl.pallas_call(kernel, name='mlp_backward', out_shape=results, in_specs=[...]
where the time goes in v3:
time: 775 us; the launch traced here: 774 us
  Pallas kernels  774 us (100%)
    pallas_call x1, Pallas kernels, fused(): pl.pallas_call(kernel, name='mlp_backward', out_shape=results, in_specs=[...  764 us

profile of v3, /device:TPU:0, one launch (start us, length us, event | category | flops | bytes accessed | tf_op | source)
XLA Modules:
  0.0 774.4 jit_solution(18035143759118576124)
XLA Ops:
  0.6 763.9 %mlp_backward.1 = (f32[3,56,4864]{2,1,0:T(8,128)}, f32[3,56,4864]{2,1,0:T(8,128)}, f32[3,304,896]{2,1,0:T(8,128)}, bf16[2048,896]{1,0:T(8,128)(2,1)}) custom-call(bf16[3,2048,896]{2,1,0:T(8,128)(2,1)} %h_hbm.1, bf16[2048,896]{1,0:T(8,128)(2,1)} %g_hbm.1, bf16[3,56,4864]{2,1,0:T(8,128)(2,1)} %w1_hbm.1, bf16[3,56,4864]{2,1,0:T(8,128)(2,1)} %w3_hbm.1, ...), custom_call_target="tpu_custom_call" | custom-call | tf_op jit(solution)/shard_map/mlp_backward/pallas_call | solution.py:482
  764.6 9.8 %hand_out.1 = (f32[3,56,4864]{2,1,0:T(8,128)}, f32[3,56,4864]{2,1,0:T(8,128)}, f32[3,304,896]{2,1,0:T(8,128)}, bf16[2048,896]{1,0:T(8,128)(2,1)}) custom-call(f32[3,56,4864]{2,1,0:T(8,128)} %get-tuple-element.8.refs_0_, f32[3,56,4864]{2,1,0:T(8,128)} %get-tuple-element.9.refs_1_, f32[3,304,896]{2,1,0:T(8,128)} %get-tuple-element.10.refs_2_, ...), custom_call_target="tpu_custom_call" | custom-call | bytes 27000000 | tf_op jit(solution)/shard_map/hand_out/pallas_call | solution.py:491

commit v4 on v3

--- a/solution.py
+++ b/solution.py
@@ -35,14 +35,14 @@
 
 
 def kernel(h_hbm, g_hbm, w1_hbm, w3_hbm, w2_hbm,
-           o1_hbm, o3_hbm, o2_hbm, og_hbm,
-           n_v, nt_v, g_v, gt_v, dn_v, h_v, a_v, d_v,
-           c1_v, c3_v, e1_v, e3_v, f1_v, f3_v, t1_v, t3_v,
+           o1_v, o3_v, o2_v, g_v,
+           n_v, nt_v, gt_v, dn_v, h_v, a_v, d_v,
+           c1_v, c3_v, e1_v, e3_v, f1_v, f3_v,
            w1_v, w3_v, w2_v,
            g1_v, g3_v, g2_v,
            rd1, rd3, rd2, ra1, ra3, ra2, rb1, rb3, rb2, rc1, rc3, rc2,
-           pa1, pa3, pa2, pb1, pb3, pb2, s1, s3, s2,
-           ag_send, ag_recv, rs_send, rs_recv, ex_send, ex_recv, own_sem, out_sem, cols_sem, h_sem, g_sem):
+           pa1, pa3, pa2, pb1, pb3, pb2, s1, s3,
+           ag_send, ag_recv, rs_send, rs_recv, ex_send, ex_recv, own_sem, cols_sem, h_sem, g_sem):
     me = lax.axis_index('fsdp')
     c = me % 2
     x = (me // 2) % 2
@@ -59,8 +59,7 @@
     weights = (w1_v, w3_v, w2_v)
     grads = (g1_v, g3_v, g2_v)
     rds, ras, rbs, rcs = (rd1, rd3, rd2), (ra1, ra3, ra2), (rb1, rb3, rb2), (rc1, rc3, rc2)
-    pas, pbs, outs = (pa1, pa3, pa2), (pb1, pb3, pb2), (t1_v, t3_v, s2)
-    dones = (s1, s3, s2)
+    pas, pbs, outs, dones = (pa1, pa3, pa2), (pb1, pb3, pb2), (o1_v, o3_v), (s1, s3)
     cols, halves, theirs = (c1_v, c3_v), (e1_v, e3_v), (f1_v, f3_v)
     order = ((nx, ny, nz), (ny, nz, nx), (nz, nx, ny))
 
@@ -89,8 +88,7 @@
         return pltpu.make_async_copy(own_rows(k), gather_slice(2, 0, k), own_sem)
 
     def cols_copy(m, li):
-        slot = lax.rem(li, 2)
-        return pltpu.make_async_copy((w1_hbm, w3_hbm)[m].at[LAYERS - 1 - li], cols[m].at[slot], cols_sem.at[m, slot])
+        return pltpu.make_async_copy((w1_hbm, w3_hbm)[m].at[LAYERS - 1 - li], cols[m], cols_sem.at[m])
 
     def half_copy(m, k):
         par = lax.rem(k, 2)
@@ -106,15 +104,13 @@
         return pl.ds(pl.multiple_of(tile * LANES, LANES), LANES), col - tile * LANES
 
     def pick_columns(k):
-        li = k // NC
         i = lax.rem(k, NC)
-        slot = lax.rem(li, 2)
         for m in range(2):
             for half in range(2):
                 acc = jnp.zeros((DS, LANES), F32)
                 for q in range(DEV // 2):
                     tile, off = place(half * (DEV // 2) + q, i)
-                    part = pltpu.roll(cols[m][slot, :, tile].astype(F32), lax.rem(CPD * q + LANES - off, LANES), 1)
+                    part = pltpu.roll(cols[m][:, tile].astype(F32), lax.rem(CPD * q + LANES - off, LANES), 1)
                     acc = jnp.where((lane >= CPD * q) & (lane < CPD * (q + 1)), part, acc)
                 halves[m][half] = acc
 
@@ -126,17 +122,16 @@
             high = jnp.where(c == 0, other, mine)
             weights[m][lax.rem(k, WS), c, z, y, x] = jnp.concatenate([low, high], axis=0).astype(BF)
 
-    def put_columns(i):
+    def put_columns(k):
+        layer = lax.rem(LAYERS - (k + NC) // NC, LAYERS)
+        i = lax.rem(k + NC, NC)
         for m in range(2):
-            put_matrix(m, i)
-
-    def put_matrix(m, i):
-        for half in range(2):
-            src = dones[m][:, half * LANES:(half + 1) * LANES]
-            for q in range(DEV // 2):
-                tile, off = place(half * (DEV // 2) + q, i)
-                part = pltpu.roll(src, lax.rem(off + LANES - CPD * q, LANES), 1)
-                outs[m][:, tile] = jnp.where((lane >= off) & (lane < off + CPD), part, outs[m][:, tile])
+            for half in range(2):
+                src = dones[m][:, half * LANES:(half + 1) * LANES]
+                for q in range(DEV // 2):
+                    tile, off = place(half * (DEV // 2) + q, i)
+                    part = pltpu.roll(src, lax.rem(off + LANES - CPD * q, LANES), 1)
+                    outs[m][layer, :, tile] = jnp.where((lane >= off) & (lane < off + CPD), part, outs[m][layer, :, tile])
 
     def reduce_copy(m, stage, k):
         par = lax.rem(k, 2)
@@ -157,14 +152,6 @@
             src_ref=src, dst_ref=dst, send_sem=rs_send.at[m, stage, slot], recv_sem=rs_recv.at[m, stage, slot],
             device_id=(peer,), device_id_type=MESH)
 
-    def out_copy(m, k):
-        layer = LAYERS - 1 - k // NC
-        if m == 2:
-            dst = o2_hbm.at[layer, pl.ds(pl.multiple_of(lax.rem(k, NC) * CPD, CPD), CPD)]
-        else:
-            dst = (o1_hbm, o3_hbm)[m].at[layer]
-        return pltpu.make_async_copy(outs[m], dst, out_sem.at[m])
-
     def h_copy(li, b):
         rows = pl.ds(pl.multiple_of(b * BB, BB), BB)
         return pltpu.make_async_copy(h_hbm.at[LAYERS - 1 - li, rows], h_v.at[rows], h_sem.at[b])
@@ -191,7 +178,7 @@
         gt_v[:, rows] = g_v[rows, :].T
         dn_v[rows, :] = jnp.zeros((BB, D), F32)
 
-    def gather_step(k):
+    def gather_first(k):
         @pl.when((k >= 1) & (k <= NK))
         def _():
             for m in range(3):
@@ -202,6 +189,7 @@
             for m in range(3):
                 gather_copy(m, 3, k).wait()
 
+    def gather_rest(k):
         for lag, stage in ((1, 2), (2, 1), (3, 0)):
             @pl.when((k + lag >= 0) & (k + lag < NK))
             def _():
@@ -209,14 +197,14 @@
                     gather_copy(m, stage, k + lag).wait()
                 if stage == 0:
                     own_copy(k + lag).wait()
-
-        for lag, stage in ((1, 3), (2, 2), (3, 1), (4, 0)):
-            @pl.when((k + lag >= 0) & (k + lag < NK))
-            def _():
                 for m in range(3):
-                    gather_copy(m, stage, k + lag).start()
-                if stage == 0:
-                    own_copy(k + lag).start()
+                    gather_copy(m, stage + 1, k + lag).start()
+
+        @pl.when((k + 4 >= 0) & (k + 4 < NK))
+        def _():
+            for m in range(3):
+                gather_copy(m, 0, k + 4).start()
+            own_copy(k + 4).start()
 
         @pl.when((k <= 0) & (k > -LEAD))
         def _():
@@ -227,15 +215,10 @@
             for m in range(2):
                 half_copy(m, k + 5).start()
 
-        @pl.when(k + 5 == NC - 1)
+        @pl.when((k + 6 == NC) | (k + 6 == 2 * NC))
         def _():
             for m in range(2):
-                cols_copy(m, 2).start()
-
-        @pl.when((k + 6 == NC) | (k + 6 == 2 * NC))
-        def _():
-            for m in range(2):
-                cols_copy(m, (k + 6) // NC).wait()
+                cols_copy(m, (k + 6) // NC).start()
 
     def reduce_step(k):
         def live(lag):
@@ -243,21 +226,14 @@
 
         def finish():
             kf = k - 4
-            i = lax.rem(kf, NC)
-
-            @pl.when(kf >= 1)
-            def _():
-                out_copy(2, kf - 1).wait()
-
-            @pl.when((kf >= 1) & (i == 0))
-            def _():
-                for m in range(2):
-                    out_copy(m, kf - 1).wait()
             for m in range(3):
                 reduce_copy(m, 3, kf).wait()
             for m in range(3):
-                dones[m][...] = rcs[m][lax.rem(kf, 3)] + pbs[m][lax.rem(kf, 2), (z, x, y)[m]]
-            out_copy(2, kf).start()
+                done = rcs[m][lax.rem(kf, 3)] + pbs[m][lax.rem(kf, 2), (z, x, y)[m]]
+                if m == 2:
+                    o2_v[LAYERS - 1 - kf // NC, pl.ds(pl.multiple_of(lax.rem(kf, NC) * CPD, CPD), CPD), :] = done
+                else:
+                    dones[m][...] = done
 
         def third():
             kf = k - 3
@@ -302,6 +278,11 @@
             for m in range(2):
                 half_copy(m, k + 5).wait()
             merge_rows(k + 5)
+
+        @pl.when((k + 6 == NC) | (k + 6 == 2 * NC))
+        def _():
+            for m in range(2):
+                cols_copy(m, (k + 6) // NC).wait()
 
         @pl.when(k <= NK)
         def _():
@@ -346,7 +327,7 @@
     def grad_phase(k):
         par = lax.rem(k, 2)
         pick_columns(k + 6)
-        put_columns(lax.rem(k - 4 + NC, NC))
+        put_columns(k - 4)
         nt = nt_v[...]
         g1_v[par] = dot(nt, d_v[:, pl.ds(0, CH)], 1, 0).reshape(2, 2, 2, 2, DS, CH)
         g3_v[par] = dot(nt, d_v[:, pl.ds(CH, CH)], 1, 0).reshape(2, 2, 2, 2, DS, CH)
@@ -358,8 +339,6 @@
         h_copy(0, b).start()
     g_copy().start()
     for m in range(2):
-        cols_copy(m, 1).start()
-    for m in range(2):
         cols_copy(m, 0).wait()
     pick_columns(0)
     pl.semaphore_wait(barrier, 4)
@@ -368,7 +347,11 @@
         k = t - LEAD
         inside = (k >= 0) & (k < NK)
         last = inside & (lax.rem(k + NC, NC) == NC - 1)
-        gather_step(k)
+        gather_first(k)
+
+        @pl.when(k != 0)
+        def _():
+            gather_rest(k)
 
         @pl.when((t >= 1) & (t < LEAD))
         def _():
@@ -385,6 +368,10 @@
         def _():
             row_phase(k)
 
+        @pl.when(k == 0)
+        def _():
+            gather_rest(k)
+
         @pl.when((last & (k < NK - 1)) | (k == NK))
         def _():
             li = k // NC
@@ -398,10 +385,6 @@
                 return cc
             lax.fori_loop(0, NB, rows, 0)
 
-            @pl.when(k == NK)
-            def _():
-                pltpu.make_async_copy(g_v, og_hbm, g_sem).start()
-
         reduce_step(k)
 
         @pl.when(inside)
@@ -410,12 +393,7 @@
 
         @pl.when(k >= NK)
         def _():
-            put_columns(lax.rem(k - 4, NC))
-
-        @pl.when((k >= 4) & (lax.rem(k - 4 + NC, NC) == NC - 1))
-        def _():
-            for m in range(2):
-                out_copy(m, k - 4).start()
+            put_columns(k - 4)
 
         @pl.when(last & (k < NK - 1))
         def _():
@@ -429,28 +407,15 @@
         return carry
 
     lax.fori_loop(0, LEAD + NK + TAIL, step, 0)
-    for m in range(3):
-        out_copy(m, NK - 1).wait()
-    pltpu.make_async_copy(g_v, og_hbm, g_sem).wait()
 
 
 def hand_out(*refs):
-    srcs, dsts, bufs, sem_in, sem_out = refs[:4], refs[4:8], refs[8:12], refs[12], refs[13]
-    pieces = []
-    for j in range(4):
-        if j < 3:
-            pieces += [(j, layer) for layer in range(LAYERS)]
-        else:
-            pieces += [(j, pl.ds(q * (ROWS // 4), ROWS // 4)) for q in range(4)]
-    ins = [pltpu.make_async_copy(srcs[j].at[w], bufs[j].at[w], sem_in.at[n]) for n, (j, w) in enumerate(pieces)]
-    outs = [pltpu.make_async_copy(bufs[j].at[w], dsts[j].at[w], sem_out.at[n]) for n, (j, w) in enumerate(pieces)]
-    for copy in ins:
+    srcs, dsts, sem = refs[:4], refs[4:8], refs[8]
+    copies = [pltpu.make_async_copy(srcs[j], dsts[j], sem.at[j]) for j in range(4)]
+    for copy in copies:
         copy.start()
-    for copy, out in zip(ins, outs):
+    for copy in copies:
         copy.wait()
-        out.start()
-    for out in outs:
-        out.wait()
 
 
 def fused(h, g, w1, w3, w2):
@@ -459,18 +424,18 @@
     wide, low = (DS, CH), (CPD, D)
     three = lambda *lead: [V(lead + wide, F32), V(lead + wide, F32), V(lead + low, F32)]
     scratch = [
-        V((ROWS, D), BF), V((D, ROWS), BF), V((ROWS, D), BF), V((D, ROWS), BF),
+        V((ROWS, D), BF), V((D, ROWS), BF), V((D, ROWS), BF),
         V((ROWS, D), F32), V((ROWS, D), BF), V((ROWS, CH), BF), V((ROWS, 2 * CH), BF),
-        V((2, DS, FF), BF), V((2, DS, FF), BF), V((2, DS, LANES), F32), V((2, DS, LANES), F32),
-        V((2, DS, LANES), F32), V((2, DS, LANES), F32), V((DS, FF), F32), V((DS, FF), F32),
+        V((DS, FF), BF), V((DS, FF), BF), V((2, DS, LANES), F32), V((2, DS, LANES), F32),
+        V((2, DS, LANES), F32), V((2, DS, LANES), F32),
         V((WS, 2, 2, 2, 2, 2 * DS, HALF), BF), V((WS, 2, 2, 2, 2, 2 * DS, HALF), BF), V((WS, 2, 2, 2, 2, CPD, D), BF),
         *three(2, 2, 2, 2, 2),
         *three(2, 2, 2, 2), *three(2, 2, 2), *three(2, 2), *three(3),
-        *three(2, 2, 2), *three(2, 2), *three(),
+        *three(2, 2, 2), *three(2, 2), V(wide, F32), V(wide, F32),
         pltpu.SemaphoreType.DMA((3, 4, 2)), pltpu.SemaphoreType.DMA((3, 4, 2)),
         pltpu.SemaphoreType.DMA((3, 4, 3)), pltpu.SemaphoreType.DMA((3, 4, 3)),
         pltpu.SemaphoreType.DMA((2, 2)), pltpu.SemaphoreType.DMA((2, 2)),
-        pltpu.SemaphoreType.DMA(()), pltpu.SemaphoreType.DMA((3,)), pltpu.SemaphoreType.DMA((2, 2)),
+        pltpu.SemaphoreType.DMA(()), pltpu.SemaphoreType.DMA((2,)),
         pltpu.SemaphoreType.DMA((NB,)), pltpu.SemaphoreType.DMA(()),
     ]
     results = (
@@ -479,25 +444,25 @@
         jax.ShapeDtypeStruct((LAYERS, FS, D), F32),
         jax.ShapeDtypeStruct((ROWS, D), BF),
     )
+    vmem_spec = pl.BlockSpec(memory_space=pltpu.VMEM)
     parts = pl.pallas_call(
         kernel,
         name='mlp_backward',
-        out_shape=results,
+        out_shape=tuple(V(r.shape, r.dtype) for r in results),
         in_specs=[any_spec] * 5,
-        out_specs=(any_spec,) * 4,
+        out_specs=(vmem_spec,) * 4,
         scratch_shapes=scratch,
-        compiler_params=pltpu.CompilerParams(collective_id=0, has_side_effects=True, vmem_limit_bytes=67_043_328),
+        compiler_params=pltpu.CompilerParams(collective_id=0, has_side_effects=True, vmem_limit_bytes=51 * 1024 * 1024),
     )(h, g, w1, w3, w2)
     return pl.pallas_call(
         hand_out,
         name='hand_out',
         out_shape=results,
-        in_specs=[any_spec] * 4,
+        in_specs=[vmem_spec] * 4,
         out_specs=(any_spec,) * 4,
-        scratch_shapes=[V(r.shape, r.dtype) for r in results] + [pltpu.SemaphoreType.DMA((13,)), pltpu.SemaphoreType.DMA((13,))],
-        compiler_params=pltpu.CompilerParams(vmem_limit_bytes=67_043_328),
-        cost_estimate=pl.CostEstimate(flops=0, bytes_accessed=27_000_000, transcendentals=0),
-    )(*parts)
+        scratch_shapes=[pltpu.SemaphoreType.DMA((4,))],
+        compiler_params=pltpu.CompilerParams(vmem_limit_bytes=1024 * 1024),
+    )(*[pltpu.with_memory_space_constraint(part, pltpu.VMEM) for part in parts])
 
 
 def solution(mesh):

time: 775 us -> 769 us (level)
  no operation moved by 1% of the time
where the time goes in v4:
time: 769 us
  Pallas kernels  768 us (100%)
    pallas_call x1, Pallas kernels, fused(): pl.pallas_call(kernel, name='mlp_backward', out_shape=tuple((V(r.shape, r...  763 us

profile of v4, /device:TPU:0, one launch (start us, length us, event | category | flops | bytes accessed | tf_op | source)
XLA Modules:
  0.0 768.7 jit_solution(15366629016119169438)
XLA Ops:
  0.6 763.1 %mlp_backward.1 = (f32[3,56,4864]{2,1,0:T(8,128)S(1)}, f32[3,56,4864]{2,1,0:T(8,128)S(1)}, f32[3,304,896]{2,1,0:T(8,128)S(1)}, bf16[2048,896]{1,0:T(8,128)(2,1)S(1)}) custom-call(bf16[3,2048,896]{2,1,0:T(8,128)(2,1)} %h_hbm.1, bf16[2048,896]{1,0:T(8,128)(2,1)} %g_hbm.1, bf16[3,56,4864]{2,1,0:T(8,128)(2,1)} %w1_hbm.1, bf16[3,56,4864]{2,1,0:T(8,128)(2,1)} %w3_hbm.1, ...), custom_call_target="tpu_custom_call" | custom-call | tf_op jit(solution)/shard_map/mlp_backward/pallas_call | solution.py:448
  763.7 5.0 hand_out.1

commit v5 on v4

--- a/solution.py
+++ b/solution.py
@@ -25,6 +25,7 @@
 HALF = CH // 2
 LANES = 128
 NB = ROWS // BB
+HR = 4
 MESH = pl.DeviceIdType.MESH
 BF = jnp.bfloat16
 F32 = jnp.float32
@@ -93,7 +94,7 @@
     def half_copy(m, k):
         par = lax.rem(k, 2)
         return pltpu.make_async_remote_copy(
-            src_ref=halves[m].at[1 - c], dst_ref=theirs[m].at[par], send_sem=ex_send.at[m, par], recv_sem=ex_recv.at[m, par],
+            src_ref=halves[m].at[par, 1 - c], dst_ref=theirs[m].at[par], send_sem=ex_send.at[m, par], recv_sem=ex_recv.at[m, par],
             device_id=(core,), device_id_type=MESH)
 
     lane = lax.broadcasted_iota(jnp.int32, (DS, LANES), 1)
@@ -112,12 +113,12 @@
                     tile, off = place(half * (DEV // 2) + q, i)
                     part = pltpu.roll(cols[m][:, tile].astype(F32), lax.rem(CPD * q + LANES - off, LANES), 1)
                     acc = jnp.where((lane >= CPD * q) & (lane < CPD * (q + 1)), part, acc)
-                halves[m][half] = acc
+                halves[m][lax.rem(k, 2), half] = acc
 
     def merge_rows(k):
         par = lax.rem(k, 2)
         for m in range(2):
-            mine, other = halves[m][c], theirs[m][par]
+            mine, other = halves[m][par, c], theirs[m][par]
             low = jnp.where(c == 0, mine, other)
             high = jnp.where(c == 0, other, mine)
             weights[m][lax.rem(k, WS), c, z, y, x] = jnp.concatenate([low, high], axis=0).astype(BF)
@@ -135,48 +136,51 @@
 
     def reduce_copy(m, stage, k):
         par = lax.rem(k, 2)
-        slot = lax.rem(k, 3) if stage == 3 else par
+        slot = par if stage == 0 else lax.rem(k, 3)
         g, pa, pb = grads[m], pas[m].at[par], pbs[m].at[par]
         if stage == 0:
             src, dst, peer = g.at[par, :, :, :, 1 - c], rds[m].at[par], core
         elif stage == 1:
             src = (g.at[par, :, :, 1 - x, c], g.at[par, :, 1 - y, :, c], g.at[par, 1 - z, :, :, c])[m]
-            dst, peer = ras[m].at[par], order[m][0]
+            dst, peer = ras[m].at[slot], order[m][0]
         elif stage == 2:
             src = (pa.at[:, 1 - y], pa.at[1 - z], pa.at[:, 1 - x])[m]
-            dst, peer = rbs[m].at[par], order[m][1]
+            dst, peer = rbs[m].at[slot], order[m][1]
         else:
             src = (pb.at[1 - z], pb.at[1 - x], pb.at[1 - y])[m]
-            dst, peer = rcs[m].at[lax.rem(k, 3)], order[m][2]
+            dst, peer = rcs[m].at[slot], order[m][2]
         return pltpu.make_async_remote_copy(
             src_ref=src, dst_ref=dst, send_sem=rs_send.at[m, stage, slot], recv_sem=rs_recv.at[m, stage, slot],
             device_id=(peer,), device_id_type=MESH)
 
     def h_copy(li, b):
         rows = pl.ds(pl.multiple_of(b * BB, BB), BB)
-        return pltpu.make_async_copy(h_hbm.at[LAYERS - 1 - li, rows], h_v.at[rows], h_sem.at[b])
+        slot = lax.rem(b, HR)
+        return pltpu.make_async_copy(h_hbm.at[LAYERS - 1 - li, rows], h_v.at[slot], h_sem.at[slot])
 
     def g_copy():
         return pltpu.make_async_copy(g_hbm, g_v, g_sem)
 
-    def finalize_rows(r0):
-        rows = pl.ds(r0, BB)
-        hf = h_v[rows, :].astype(F32)
+    def finalize_rows(b):
+        rows = pl.ds(pl.multiple_of(b * BB, BB), BB)
+        hf = h_v[lax.rem(b, HR)].astype(F32)
         r = lax.rsqrt(jnp.mean(hf * hf, axis=-1, keepdims=True) + EPS)
         m = hf * r
         dn = dn_v[rows, :]
         dr = r * (dn - m * jnp.mean(dn * m, axis=-1, keepdims=True))
         g_v[rows, :] = (g_v[rows, :].astype(F32) + dr).astype(BF)
 
-    def prepare_rows(r0):
-        rows = pl.ds(r0, BB)
-        hf = h_v[rows, :].astype(F32)
+    def prepare_rows(li, b):
+        rows = pl.ds(pl.multiple_of(b * BB, BB), BB)
+        h_copy(li, b).wait()
+        hf = h_v[lax.rem(b, HR)].astype(F32)
         r = lax.rsqrt(jnp.mean(hf * hf, axis=-1, keepdims=True) + EPS)
         nb = (hf * r).astype(BF)
         n_v[rows, :] = nb
         nt_v[:, rows] = nb.T
         gt_v[:, rows] = g_v[rows, :].T
         dn_v[rows, :] = jnp.zeros((BB, D), F32)
+        h_copy(li, lax.rem(b + HR, NB)).start()
 
     def gather_first(k):
         @pl.when((k >= 1) & (k <= NK))
@@ -190,6 +194,12 @@
                 gather_copy(m, 3, k).wait()
 
     def gather_rest(k):
+        @pl.when((k + 4 >= 0) & (k + 4 < NK))
+        def _():
+            for m in range(2):
+                half_copy(m, k + 4).wait()
+            merge_rows(k + 4)
+
         for lag, stage in ((1, 2), (2, 1), (3, 0)):
             @pl.when((k + lag >= 0) & (k + lag < NK))
             def _():
@@ -243,7 +253,7 @@
             for m in range(3):
                 for a in range(2):
                     kept = (lambda: pa1[par, a, y], lambda: pa3[par, z, a], lambda: pa2[par, a, x])[m]()
-                    pbs[m][par, a] = rbs[m][par, a] + kept
+                    pbs[m][par, a] = rbs[m][lax.rem(kf, 3), a] + kept
             for m in range(3):
                 reduce_copy(m, 3, kf).start()
 
@@ -256,7 +266,7 @@
                 for a in range(2):
                     for b in range(2):
                         kept = (lambda: g1_v[par, a, b, x, c], lambda: g3_v[par, a, y, b, c], lambda: g2_v[par, z, a, b, c])[m]()
-                        pas[m][par, a, b] = ras[m][par, a, b] + kept
+                        pas[m][par, a, b] = ras[m][lax.rem(kf, 3), a, b] + kept
             for m in range(3):
                 reduce_copy(m, 2, kf).start()
 
@@ -273,26 +283,21 @@
             for m in range(3):
                 reduce_copy(m, 1, kf).start()
 
-        @pl.when(k + 5 < NK)
-        def _():
-            for m in range(2):
-                half_copy(m, k + 5).wait()
-            merge_rows(k + 5)
-
         @pl.when((k + 6 == NC) | (k + 6 == 2 * NC))
         def _():
             for m in range(2):
                 cols_copy(m, (k + 6) // NC).wait()
 
-        @pl.when(k <= NK)
+        @pl.when(k < NK)
         def _():
             pl.when(live(4))(finish)
             pl.when(live(3))(third)
             pl.when(live(2))(second)
             pl.when(live(1))(first)
 
-        @pl.when(k > NK)
-        def _():
+        @pl.when(k >= NK)
+        def _():
+            pl.when(live(1))(first)
             pl.when(live(2))(second)
             pl.when(live(3))(third)
             pl.when(live(4))(finish)
@@ -301,6 +306,10 @@
         s = lax.rem(k, WS)
 
         def body(b, carry):
+            @pl.when((k == 0) & (b == 1))
+            def _():
+                gather_rest(k)
+
             rows = pl.ds(pl.multiple_of(b * RB, RB), RB)
             w1 = jnp.concatenate([w1_v[s, 0].reshape(D, HALF), w1_v[s, 1].reshape(D, HALF)], axis=1)
             w3 = jnp.concatenate([w3_v[s, 0].reshape(D, HALF), w3_v[s, 1].reshape(D, HALF)], axis=1)
@@ -335,7 +344,7 @@
 
     for m in range(2):
         cols_copy(m, 0).start()
-    for b in range(NB):
+    for b in range(HR):
         h_copy(0, b).start()
     g_copy().start()
     for m in range(2):
@@ -357,31 +366,30 @@
         def _():
             @pl.when(t == 1)
             def _():
-                for b in range(NB):
-                    h_copy(0, b).wait()
                 g_copy().wait()
             per = NB // (LEAD - 1)
             for j in range(per):
-                prepare_rows(pl.multiple_of(((t - 1) * per + j) * BB, BB))
+                prepare_rows(0, (t - 1) * per + j)
 
         @pl.when(inside)
         def _():
             row_phase(k)
 
-        @pl.when(k == 0)
-        def _():
-            gather_rest(k)
-
         @pl.when((last & (k < NK - 1)) | (k == NK))
         def _():
-            li = k // NC
+            li = (k - 1) // NC
 
             def rows(b, cc):
-                finalize_rows(pl.multiple_of(b * BB, BB))
-
-                @pl.when(k < NK)
+                h_copy(li, b).wait()
+                finalize_rows(b)
+
+                @pl.when(b < NB - HR)
                 def _():
-                    h_copy(li + 1, b).start()
+                    h_copy(li, b + HR).start()
+
+                @pl.when((b >= NB - HR) & (k < NK))
+                def _():
+                    h_copy(li + 1, b + HR - NB).start()
                 return cc
             lax.fori_loop(0, NB, rows, 0)
 
@@ -400,8 +408,7 @@
             li = k // NC
 
             def rows(b, cc):
-                h_copy(li + 1, b).wait()
-                prepare_rows(pl.multiple_of(b * BB, BB))
+                prepare_rows(li + 1, b)
                 return cc
             lax.fori_loop(0, NB, rows, 0)
         return carry
@@ -411,7 +418,9 @@
 
 def hand_out(*refs):
     srcs, dsts, sem = refs[:4], refs[4:8], refs[8]
-    copies = [pltpu.make_async_copy(srcs[j], dsts[j], sem.at[j]) for j in range(4)]
+    pieces = [(j, layer) for j in range(3) for layer in range(LAYERS)]
+    pieces += [(3, pl.ds(q * (ROWS // 4), ROWS // 4)) for q in range(4)]
+    copies = [pltpu.make_async_copy(srcs[j].at[w], dsts[j].at[w], sem.at[n]) for n, (j, w) in enumerate(pieces)]
     for copy in copies:
         copy.start()
     for copy in copies:
@@ -425,18 +434,18 @@
     three = lambda *lead: [V(lead + wide, F32), V(lead + wide, F32), V(lead + low, F32)]
     scratch = [
         V((ROWS, D), BF), V((D, ROWS), BF), V((D, ROWS), BF),
-        V((ROWS, D), F32), V((ROWS, D), BF), V((ROWS, CH), BF), V((ROWS, 2 * CH), BF),
-        V((DS, FF), BF), V((DS, FF), BF), V((2, DS, LANES), F32), V((2, DS, LANES), F32),
+        V((ROWS, D), F32), V((HR, BB, D), BF), V((ROWS, CH), BF), V((ROWS, 2 * CH), BF),
+        V((DS, FF), BF), V((DS, FF), BF), V((2, 2, DS, LANES), F32), V((2, 2, DS, LANES), F32),
         V((2, DS, LANES), F32), V((2, DS, LANES), F32),
         V((WS, 2, 2, 2, 2, 2 * DS, HALF), BF), V((WS, 2, 2, 2, 2, 2 * DS, HALF), BF), V((WS, 2, 2, 2, 2, CPD, D), BF),
         *three(2, 2, 2, 2, 2),
-        *three(2, 2, 2, 2), *three(2, 2, 2), *three(2, 2), *three(3),
+        *three(2, 2, 2, 2), *three(3, 2, 2), *three(3, 2), *three(3),
         *three(2, 2, 2), *three(2, 2), V(wide, F32), V(wide, F32),
         pltpu.SemaphoreType.DMA((3, 4, 2)), pltpu.SemaphoreType.DMA((3, 4, 2)),
         pltpu.SemaphoreType.DMA((3, 4, 3)), pltpu.SemaphoreType.DMA((3, 4, 3)),
         pltpu.SemaphoreType.DMA((2, 2)), pltpu.SemaphoreType.DMA((2, 2)),
         pltpu.SemaphoreType.DMA(()), pltpu.SemaphoreType.DMA((2,)),
-        pltpu.SemaphoreType.DMA((NB,)), pltpu.SemaphoreType.DMA(()),
+        pltpu.SemaphoreType.DMA((HR,)), pltpu.SemaphoreType.DMA(()),
     ]
     results = (
         jax.ShapeDtypeStruct((LAYERS, DS, FF), F32),
@@ -460,7 +469,7 @@
         out_shape=results,
         in_specs=[vmem_spec] * 4,
         out_specs=(any_spec,) * 4,
-        scratch_shapes=[pltpu.SemaphoreType.DMA((4,))],
+        scratch_shapes=[pltpu.SemaphoreType.DMA((13,))],
         compiler_params=pltpu.CompilerParams(vmem_limit_bytes=1024 * 1024),
     )(*[pltpu.with_memory_space_constraint(part, pltpu.VMEM) for part in parts])
 

time: 769 us -> 763 us (level)
  no operation moved by 1% of the time
where the time goes in v5:
time: 763 us
  Pallas kernels  763 us (100%)
    pallas_call x1, Pallas kernels, fused(): pl.pallas_call(kernel, name='mlp_backward', out_shape=tuple((V(r.shape, r...  758 us

profile of v5, /device:TPU:0, one launch (start us, length us, event | category | flops | bytes accessed | tf_op | source)
XLA Modules:
  0.0 763.4 jit_solution(7290804766285607327)
XLA Ops:
  0.6 757.8 %mlp_backward.1 = (f32[3,56,4864]{2,1,0:T(8,128)S(1)}, f32[3,56,4864]{2,1,0:T(8,128)S(1)}, f32[3,304,896]{2,1,0:T(8,128)S(1)}, bf16[2048,896]{1,0:T(8,128)(2,1)S(1)}) custom-call(bf16[3,2048,896]{2,1,0:T(8,128)(2,1)} %h_hbm.1, bf16[2048,896]{1,0:T(8,128)(2,1)} %g_hbm.1, bf16[3,56,4864]{2,1,0:T(8,128)(2,1)} %w1_hbm.1, bf16[3,56,4864]{2,1,0:T(8,128)(2,1)} %w3_hbm.1, ...), custom_call_target="tpu_custom_call" | custom-call | tf_op jit(solution)/shard_map/mlp_backward/pallas_call | solution.py:457
  758.4 4.9 hand_out.1
